TPU v7x, 32 devices: a whole 2x2x4 slice. The times are simulated.
32 devices in a mesh: blk: 32 (over z, y, x, core).
Axes of the slice: x: 2, y: 2, z: 4, core: 2. Of those that a mesh axis runs over, the one named last changes fastest.
Arguments:
- defect: float32 [384, 128], P('blk'), may hold values from -6 to 6
- mass: float32 [384, 128], P('blk'), may hold values from 1 to 2
- block_diag: float32 [384, 128, 128], P('blk'), may hold values from -0.1875 to 0.1875
- coupling: float32 [3072, 128, 128], P('blk'), may hold values from -0.09375 to 0.09375
- tile_rows: int32 [3072], P('blk'), may hold values from 0 to 383, as said below
- tile_cols: int32 [3072], P('blk'), may hold values from 0 to 383, as said below
Outputs:
- update: float32 [384, 128], P('blk')
Inputs may be any that keep to these rules, and one draw needn't show every extreme that they name: `tile_rows`: block rows d * 12 to d * 12 + 11 belong to device d of blk, and each device holds the tiles at positions d * 96 to d * 96 + 95. Of every tile a device holds, exactly one of its block row and block column belongs to that device; the other belongs to a different device. Exactly half of the 96 tiles of every device have their block row with that device, and the other half their block column. A program may send only the blocks and products of tiles that exist; slots of a padded buffer that no tile fills need not be sent. `tile_cols`: of one device's tiles, at most 2 have their block column with any one other device and at most 2 have their block row with any one other device; every device reaches 2 with some other device on each of the two sides.
All inputs are finite; a program needn't handle non-finite values.
Results may differ from a plain program's by a relative error of at most 0.0001.
Values sent between devices are 32-bit elements; how exact they have to be, the bound alone decides.
No kernel may reach another device: no remote copies, remote signals or barrier semaphores. Data moves between devices by JAX's collectives and lax.ppermute only.
A program may use at most 64 MiB of HBM per device.

v0:
```python
import jax
import jax.numpy as jnp
from jax import lax
from jax.sharding import PartitionSpec as P

ITERS = 3


def solve_small(gram, target):
    factor = jnp.linalg.cholesky(gram)
    count = gram.shape[0]
    forward = []
    for index in range(count):
        value = target[index]
        for inner in range(index):
            value = value - factor[index, inner] * forward[inner]
        forward.append(value / factor[index, index])
    backward = [None] * count
    for index in reversed(range(count)):
        value = forward[index]
        for inner in range(index + 1, count):
            value = value - factor[inner, index] * backward[inner]
        backward[index] = value / factor[index, index]
    return backward


def tile_products(coupling, inputs):
    return jnp.einsum("tij,tj->ti", coupling, inputs, precision=lax.Precision.HIGHEST)


def row_sum(targets, values, rows_here):
    onehot = (jnp.arange(rows_here, dtype=jnp.int32)[:, None] == targets[None, :]).astype(
        jnp.float32
    )
    return jnp.dot(
        onehot, values, precision=lax.Precision.HIGHEST, preferred_element_type=jnp.float32
    )


def lane_slots(lanes, lane_count):
    onehot = (lanes[:, None] == jnp.arange(lane_count, dtype=jnp.int32)[None, :]).astype(jnp.int32)
    before = jnp.cumsum(onehot, axis=0) - onehot
    return jnp.sum(before * onehot, axis=1)


def on_device(defect, mass, block_diag, coupling, tile_rows, tile_cols):
    rows_here = defect.shape[0]
    width = defect.shape[1]
    tiles_here = tile_rows.shape[0]
    devices = lax.axis_size("blk")
    slots = (tiles_here // 2 + devices - 2) // (devices - 1)
    myself = lax.axis_index("blk")
    row_owner = tile_rows // rows_here
    col_owner = tile_cols // rows_here
    row_local = tile_rows % rows_here
    col_local = tile_cols % rows_here
    fetch_need = col_owner != myself
    push_need = row_owner != myself
    fetch_lane = jnp.where(fetch_need, col_owner, devices)
    push_lane = jnp.where(push_need, row_owner, devices)
    fetch_slot = lane_slots(fetch_lane, devices)
    push_slot = lane_slots(push_lane, devices)
    requests = (
        jnp.zeros((devices, slots), jnp.int32)
        .at[fetch_lane, fetch_slot]
        .set(col_local, mode="drop")
    )
    targets = (
        jnp.zeros((devices, slots), jnp.int32).at[push_lane, push_slot].set(row_local, mode="drop")
    )
    asked, landing = (
        lax.all_to_all(requests, "blk", split_axis=0, concat_axis=0, tiled=True),
        lax.all_to_all(targets, "blk", split_axis=0, concat_axis=0, tiled=True),
    )
    fetch_pick = jnp.minimum(fetch_lane, devices - 1)
    kept_rows = jnp.where(push_need, -1, row_local)
    landing_flat = landing.reshape(-1)
    negated = -defect
    beta = jnp.sqrt(lax.psum(jnp.sum(negated * negated), "blk"))
    basis = [negated / beta]
    upper = jnp.zeros((ITERS + 1, ITERS), jnp.float32)
    for column in range(ITERS):
        apply_vector = basis[column]
        fetched = lax.all_to_all(
            apply_vector[asked], "blk", split_axis=0, concat_axis=0, tiled=True
        )
        inputs = jnp.where(
            fetch_need[:, None], fetched[fetch_pick, fetch_slot], apply_vector[col_local]
        )
        products = tile_products(coupling, inputs)
        outgoing = (
            jnp.zeros((devices, slots, width), jnp.float32)
            .at[push_lane, push_slot]
            .set(products, mode="drop")
        )
        arrived = lax.all_to_all(outgoing, "blk", split_axis=0, concat_axis=0, tiled=True)
        local_rows = row_sum(kept_rows, products, rows_here)
        remote_rows = row_sum(landing_flat, arrived.reshape(-1, width), rows_here)
        own = jnp.einsum("rij,rj->ri", block_diag, apply_vector, precision=lax.Precision.HIGHEST)
        image = mass * apply_vector + own + local_rows + remote_rows
        local_dots = jnp.stack([jnp.sum(item * image) for item in basis])
        dots = lax.psum(local_dots, "blk")
        for index in range(column + 1):
            image = image - dots[index] * basis[index]
        norm = jnp.sqrt(lax.psum(jnp.sum(image * image), "blk"))
        upper = upper.at[: column + 1, column].set(dots)
        upper = upper.at[column + 1, column].set(norm)
        if column + 1 < ITERS:
            basis.append(image / norm)
    gram = jnp.dot(
        upper.T, upper, precision=lax.Precision.HIGHEST, preferred_element_type=jnp.float32
    )
    mixing = solve_small(gram, beta * upper[0, :])
    update = jnp.zeros_like(defect)
    for index in range(ITERS):
        update = update + mixing[index] * basis[index]
    return update


def solution(mesh):
    in_specs = (
        P("blk", None),
        P("blk", None),
        P("blk", None, None),
        P("blk", None, None),
        P("blk"),
        P("blk"),
    )
    out_specs = P("blk", None)
    return jax.shard_map(
        on_device, mesh=mesh, in_specs=in_specs, out_specs=out_specs, check_vma=False
    )
```

profile of v0, /device:TPU:0, one launch (start us, length us, event | category | flops | bytes accessed | tf_op | source)
XLA Modules:
  0.0 493.8 jit_solution(12215149020119974177)
XLA Ops:
  2.5 5.0 %scatter_fusion = s32[32,2]{0,1:T(2,128)S(1)} fusion(s32[32,2]{0,1:T(2,128)S(1)} %broadcast.206.clone, s32[96]{0:T(128)S(1)} %get-tuple-element.102, s32[96]{0:T(128)S(1)} %get-tuple-element.91), kind=kCustom, calls=%fused_computation.9 | custom fusion | bytes 1920 | tf_op jit(solution)/shard_map/scatter | solution.py:66
  8.2 1.3 multiply_reduce_fusion.9
  9.5 7.3 %all-to-all-start = ((s32[32,1,2]{2,1,0:T(1,128)}), s32[32,1,2]{2,1,0:T(1,128)S(1)}, u32[]{:S(2)}, u32[]{:S(2)}) async-start(s32[32,1,2]{2,1,0:T(1,128)} %copy.13), calls=%async_computation | async-start | bytes 32768 | tf_op jit(solution)/shard_map/all_to_all | solution.py:72
  16.8 40.7 %psum.49 = f32[]{:T(128)} all-reduce(f32[]{:T(128)} %multiply_reduce_fusion.9), channel_id=1, replica_groups=mesh['blk'=32] {'blk'}, use_global_device_ids=true, to_apply=%region_1.2 | all-reduce | flops 1 | bytes 8 | tf_op jit(solution)/shard_map/psum | solution.py:79
  61.3 1.4 and_reduce_fusion
  62.7 1.3 fusion.6
  64.0 5.0 %scatter_fusion.1 = s32[32,2]{0,1:T(2,128)S(1)} fusion(s32[32,2]{0,1:T(2,128)S(1)} %broadcast.206.clone.1, s32[96]{0:T(128)S(1)} %fusion.24, s32[96]{0:T(128)S(1)} %get-tuple-element.87), kind=kCustom, calls=%fused_computation.10 | custom fusion | bytes 1920 | tf_op jit(solution)/shard_map/scatter | solution.py:69
  70.3 4.7 all-to-all-start.2
  75.3 1.2 gather_fusion
  76.5 5.7 %all-to-all-done.2 = s32[32,1,2]{2,1,0:T(1,128)S(1)} async-done(((s32[32,1,2]{2,1,0:T(1,128)}), s32[32,1,2]{2,1,0:T(1,128)S(1)}, u32[]{:S(2)}, u32[]{:S(2)}) %all-to-all-start.2) | async-done | bytes 288 | tf_op jit(solution)/shard_map/all_to_all | solution.py:73
  82.2 2.6 all-to-all-start.1
  86.7 5.3 %all-to-all-done.1 = f32[32,2,128]{2,1,0:T(2,128)S(1)} async-done(((f32[32,2,128]{2,1,0:T(2,128)}), f32[32,2,128]{2,1,0:T(2,128)S(1)}, u32[]{:S(2)}, u32[]{:S(2)}) %all-to-all-start.1) | async-done | bytes 32800 | tf_op jit(solution)/shard_map/all_to_all | solution.py:84
  92.0 1.2 gather_fusion.1
  93.3 11.8 %fusion.32 = f32[96,1,128]{2,1,0:T(1,128)S(1)} fusion(f32[96,128,1]{1,2,0:T(1,128)S(1)} %bitcast.142, f32[96,128,128]{2,1,0:T(8,128)} %param.21), kind=kOutput, calls=%fused_computation.117 | convolution fusion | flops 18874368 | bytes 6389760 | tf_op jit(solution)/shard_map/tij,tj->ti/dot_general | solution.py:28
  105.8 11.3 %scatter_fusion.2 = f32[32,2,128]{2,1,0:T(2,128)} fusion(f32[32,2,128]{2,1,0:T(2,128)} %broadcast.211.clone, s32[96]{0:T(128)S(1)} %fusion.24, f32[96,128]{1,0:T(8,128)S(1)} %bitcast.137), kind=kCustom, calls=%fused_computation.11 | custom fusion | bytes 148224 | tf_op jit(solution)/shard_map/scatter | solution.py:94
  117.2 2.6 all-to-all-start.3
  119.9 7.1 %all-to-all-done.3 = f32[32,2,128]{2,1,0:T(2,128)S(1)} async-done(((f32[32,2,128]{2,1,0:T(2,128)}), f32[32,2,128]{2,1,0:T(2,128)S(1)}, u32[]{:S(2)}, u32[]{:S(2)}) %all-to-all-start.3) | async-done | bytes 32800 | tf_op jit(solution)/shard_map/all_to_all | solution.py:96
  127.7 38.4 %psum.50 = f32[1]{0:T(128)} all-reduce(f32[1]{0:T(128)} %bitcast.19), channel_id=1, replica_groups=mesh['blk'=32] {'blk'}, use_global_device_ids=true, to_apply=%region_10.11 | all-reduce | flops 1 | bytes 8 | tf_op jit(solution)/shard_map/psum | solution.py:102
  166.2 1.3 multiply_reduce_fusion.7
  168.1 40.4 %psum.51 = f32[]{:T(128)} all-reduce(f32[]{:T(128)} %multiply_reduce_fusion.7), channel_id=1, replica_groups=mesh['blk'=32] {'blk'}, use_global_device_ids=true, to_apply=%region_12.13 | all-reduce | flops 1 | bytes 8 | tf_op jit(solution)/shard_map/psum | solution.py:105
  211.1 5.0 %all-to-all-start.4 = ((f32[32,2,128]{2,1,0:T(2,128)}), f32[32,2,128]{2,1,0:T(2,128)S(1)}, u32[]{:S(2)}, u32[]{:S(2)}) async-start(f32[32,2,128]{2,1,0:T(2,128)} %bitcast.25), calls=%async_computation.4 | async-start | bytes 65536 | tf_op jit(solution)/shard_map/all_to_all | solution.py:84
  216.2 1.3 fusion.4
  218.8 4.5 all-to-all-done.4
  223.2 1.2 gather_fusion.4
  224.6 11.8 %fusion.33 = f32[96,1,128]{2,1,0:T(1,128)S(1)} fusion(f32[96,128,1]{1,2,0:T(1,128)S(1)} %bitcast.143, f32[96,128,128]{2,1,0:T(8,128)} %param.21), kind=kOutput, calls=%fused_computation.118 | convolution fusion | flops 18874368 | bytes 6389760 | tf_op jit(solution)/shard_map/tij,tj->ti/dot_general | solution.py:28
  237.0 11.3 %scatter_fusion.3 = f32[32,2,128]{2,1,0:T(2,128)} fusion(f32[32,2,128]{2,1,0:T(2,128)} %broadcast.211.clone.1, s32[96]{0:T(128)S(1)} %fusion.24, f32[96,128]{1,0:T(8,128)S(1)} %bitcast.139), kind=kCustom, calls=%fused_computation.12 | custom fusion | bytes 148224 | tf_op jit(solution)/shard_map/scatter | solution.py:94
  248.4 2.6 all-to-all-start.5
  251.1 7.1 %all-to-all-done.5 = f32[32,2,128]{2,1,0:T(2,128)S(1)} async-done(((f32[32,2,128]{2,1,0:T(2,128)}), f32[32,2,128]{2,1,0:T(2,128)S(1)}, u32[]{:S(2)}, u32[]{:S(2)}) %all-to-all-start.5) | async-done | bytes 32800 | tf_op jit(solution)/shard_map/all_to_all | solution.py:96
  259.0 1.4 pad_maximum_fusion
  260.6 38.3 %psum.52 = f32[2]{0:T(128)S(1)} all-reduce(f32[2]{0:T(128)S(1)} %pad_maximum_fusion), channel_id=1, replica_groups=mesh['blk'=32] {'blk'}, use_global_device_ids=true, to_apply=%region_17.18 | all-reduce | flops 2 | bytes 16 | tf_op jit(solution)/shard_map/psum | solution.py:102
  299.5 2.0 multiply_reduce_fusion.4
  301.5 40.2 %psum.53 = f32[]{:T(128)} all-reduce(f32[]{:T(128)} %get-tuple-element.82), channel_id=1, replica_groups=mesh['blk'=32] {'blk'}, use_global_device_ids=true, to_apply=%region_19.20 | all-reduce | flops 1 | bytes 8 | tf_op jit(solution)/shard_map/psum | solution.py:105
  343.6 5.0 %all-to-all-start.6 = ((f32[32,2,128]{2,1,0:T(2,128)}), f32[32,2,128]{2,1,0:T(2,128)S(1)}, u32[]{:S(2)}, u32[]{:S(2)}) async-start(f32[32,2,128]{2,1,0:T(2,128)} %bitcast.41), calls=%async_computation.6 | async-start | bytes 65536 | tf_op jit(solution)/shard_map/all_to_all | solution.py:84
  348.6 1.3 fusion.2
  350.0 1.8 broadcast_select_fusion.4
  352.4 3.3 all-to-all-done.6
  355.7 1.2 gather_fusion.7
  357.0 11.8 %fusion.34 = f32[96,1,128]{2,1,0:T(1,128)S(1)} fusion(f32[96,128,1]{1,2,0:T(1,128)S(1)} %bitcast.141, f32[96,128,128]{2,1,0:T(8,128)} %param.21), kind=kOutput, calls=%fused_computation.119 | convolution fusion | flops 18874368 | bytes 6389760 | tf_op jit(solution)/shard_map/tij,tj->ti/dot_general | solution.py:28
  369.5 11.3 %scatter_fusion.4 = f32[32,2,128]{2,1,0:T(2,128)} fusion(f32[32,2,128]{2,1,0:T(2,128)} %broadcast.211, s32[96]{0:T(128)S(1)} %fusion.24, f32[96,128]{1,0:T(8,128)S(1)} %bitcast.135), kind=kCustom, calls=%fused_computation.13 | custom fusion | bytes 148224 | tf_op jit(solution)/shard_map/scatter | solution.py:94
  380.8 2.6 all-to-all-start.7
  383.5 7.1 %all-to-all-done.7 = f32[32,2,128]{2,1,0:T(2,128)S(1)} async-done(((f32[32,2,128]{2,1,0:T(2,128)}), f32[32,2,128]{2,1,0:T(2,128)S(1)}, u32[]{:S(2)}, u32[]{:S(2)}) %all-to-all-start.7) | async-done | bytes 32800 | tf_op jit(solution)/shard_map/all_to_all | solution.py:96
  391.5 2.0 pad_maximum_fusion.1
  393.4 1.3 scatter.71
  394.8 38.3 %psum.54 = f32[3]{0:T(128)S(1)} all-reduce(f32[3]{0:T(128)S(1)} %pad_maximum_fusion.1), channel_id=1, replica_groups=mesh['blk'=32] {'blk'}, use_global_device_ids=true, to_apply=%region_25.26 | all-reduce | flops 3 | bytes 24 | tf_op jit(solution)/shard_map/psum | solution.py:102
  433.7 2.5 multiply_reduce_fusion
  436.3 40.2 %psum.55 = f32[]{:T(128)} all-reduce(f32[]{:T(128)} %multiply_reduce_fusion), channel_id=1, replica_groups=mesh['blk'=32] {'blk'}, use_global_device_ids=true, to_apply=%region_27.28 | all-reduce | flops 1 | bytes 8 | tf_op jit(solution)/shard_map/psum | solution.py:105
  477.3 1.9 broadcast_select_fusion.3
  479.2 1.4 scatter.74
  (76 shorter events, 25.5 us)
Async XLA Ops:
  0.0 62.7 %copy-start = (f32[12,128,128]{2,1,0:T(8,128)S(1)}, f32[12,128,128]{2,1,0:T(8,128)}, u32[]{:S(2)}) copy-start(f32[12,128,128]{2,1,0:T(8,128)} %param.20) | copy-start | bytes 2359300
  0.0 119.7 %copy-start.2 = (f32[12,128]{1,0:T(8,128)S(1)}, f32[12,128]{1,0:T(8,128)}, u32[]{:S(2)}) copy-start(f32[12,128]{1,0:T(8,128)} %param.19) | copy-start | bytes 18436
  2.3 163.9 %copy-start.1 = (f32[12,128]{1,0:T(8,128)S(1)}, f32[12,128]{1,0:T(8,128)}, u32[]{:S(2)}) copy-start(f32[12,128]{1,0:T(8,128)} %param.18) | copy-start | bytes 18436
  9.5 60.8 %all-to-all-start = ((s32[32,1,2]{2,1,0:T(1,128)}), s32[32,1,2]{2,1,0:T(1,128)S(1)}, u32[]{:S(2)}, u32[]{:S(2)}) async-start(s32[32,1,2]{2,1,0:T(1,128)} %copy.13), calls=%async_computation | async-start | bytes 32768 | tf_op jit(solution)/shard_map/all_to_all | solution.py:72
  70.3 11.9 %all-to-all-start.2 = ((s32[32,1,2]{2,1,0:T(1,128)}), s32[32,1,2]{2,1,0:T(1,128)S(1)}, u32[]{:S(2)}, u32[]{:S(2)}) async-start(s32[32,1,2]{2,1,0:T(1,128)} %copy.16), calls=%async_computation.2 | async-start | bytes 32768 | tf_op jit(solution)/shard_map/all_to_all | solution.py:73
  82.2 9.8 %all-to-all-start.1 = ((f32[32,2,128]{2,1,0:T(2,128)}), f32[32,2,128]{2,1,0:T(2,128)S(1)}, u32[]{:S(2)}, u32[]{:S(2)}) async-start(f32[32,2,128]{2,1,0:T(2,128)} %bitcast.7), calls=%async_computation.1 | async-start | bytes 65536 | tf_op jit(solution)/shard_map/all_to_all | solution.py:84
  117.2 9.8 %all-to-all-start.3 = ((f32[32,2,128]{2,1,0:T(2,128)}), f32[32,2,128]{2,1,0:T(2,128)S(1)}, u32[]{:S(2)}, u32[]{:S(2)}) async-start(f32[32,2,128]{2,1,0:T(2,128)} %scatter_fusion.2), calls=%async_computation.3 | async-start | bytes 65536 | tf_op jit(solution)/shard_map/all_to_all | solution.py:96
  211.1 12.1 %all-to-all-start.4 = ((f32[32,2,128]{2,1,0:T(2,128)}), f32[32,2,128]{2,1,0:T(2,128)S(1)}, u32[]{:S(2)}, u32[]{:S(2)}) async-start(f32[32,2,128]{2,1,0:T(2,128)} %bitcast.25), calls=%async_computation.4 | async-start | bytes 65536 | tf_op jit(solution)/shard_map/all_to_all | solution.py:84
  248.4 9.8 %all-to-all-start.5 = ((f32[32,2,128]{2,1,0:T(2,128)}), f32[32,2,128]{2,1,0:T(2,128)S(1)}, u32[]{:S(2)}, u32[]{:S(2)}) async-start(f32[32,2,128]{2,1,0:T(2,128)} %scatter_fusion.3), calls=%async_computation.5 | async-start | bytes 65536 | tf_op jit(solution)/shard_map/all_to_all | solution.py:96
  343.6 12.0 %all-to-all-start.6 = ((f32[32,2,128]{2,1,0:T(2,128)}), f32[32,2,128]{2,1,0:T(2,128)S(1)}, u32[]{:S(2)}, u32[]{:S(2)}) async-start(f32[32,2,128]{2,1,0:T(2,128)} %bitcast.41), calls=%async_computation.6 | async-start | bytes 65536 | tf_op jit(solution)/shard_map/all_to_all | solution.py:84
  380.8 9.8 %all-to-all-start.7 = ((f32[32,2,128]{2,1,0:T(2,128)}), f32[32,2,128]{2,1,0:T(2,128)S(1)}, u32[]{:S(2)}, u32[]{:S(2)}) async-start(f32[32,2,128]{2,1,0:T(2,128)} %scatter_fusion.4), calls=%async_computation.7 | async-start | bytes 65536 | tf_op jit(solution)/shard_map/all_to_all | solution.py:96
where the time goes:
time: 496 us; the launch traced here: 494 us
  blocking collectives  277 us (56%)
  local copies, waits for them, and re-layouts  64.7 us (13%)
  matrix products  42.4 us (9%)
  waiting for transfers between devices  40.1 us (8%)
  starting transfers between devices  32.3 us (7%)
  other arithmetic  25.1 us (5%)
  between operations  12.6 us (3%)
    psum x3, blocking collectives, on_device(): norm = jnp.sqrt(lax.psum(jnp.sum(image * image), 'blk'))  121 us
    psum x3, blocking collectives, on_device(): dots = lax.psum(local_dots, 'blk')  115 us
    psum x1, blocking collectives, on_device(): beta = jnp.sqrt(lax.psum(jnp.sum(negated * negated), 'blk'))  40.7 us
    dot_general x3, matrix products, tile_products(): jnp.einsum('tij,tj->ti', coupling, inputs, precision=lax.Precision.HIGHEST)  35.5 us
    scatter x3, local copies, waits for them, and re-layouts, on_device(): outgoing = jnp.zeros((devices, slots, width), jnp.float32).at[push_lane,...  34 us
    all_to_all x3, waiting for transfers between devices, on_device(): lax.all_to_all(outgoing, 'blk', split_axis=0, concat_axis=0, tiled=True)  21.4 us
    all_to_all x3, waiting for transfers between devices, on_device(): lax.all_to_all(apply_vector[asked], 'blk', split_axis=0, concat_axis=0, t...  13.1 us
    all_to_all x3, starting transfers between devices, on_device(): lax.all_to_all(apply_vector[asked], 'blk', split_axis=0, concat_axis=0, t...  12.6 us
  transfers between devices with their start and end apart: 8, of which 7 were waited for; matrix products, arithmetic and copies ran while one was open for 4% of the time, Pallas kernels for 0%

commit v1 on v0

v1 whole, which is shorter than its diff:
```python
import functools

import jax
import jax.numpy as jnp
from jax import lax
from jax.experimental import pallas as pl
from jax.experimental.pallas import tpu as pltpu
from jax.sharding import PartitionSpec as P

F32 = jnp.float32
BF16 = jnp.bfloat16
NT = (((1,), (1,)), ((), ()))
NN = (((1,), (0,)), ((), ()))
TN = (((0,), (0,)), ((), ()))
FLOOR = 2.0**-22
MIB = 1 << 20


def round_up(value, step):
    return -(-value // step) * step


class Sizes:
    def __init__(self, devices, rows, width, tiles):
        self.devices = devices
        self.rows = rows
        self.width = width
        self.tiles = tiles
        self.half = tiles // 2
        self.slots = (self.half + devices - 2) // (devices - 1)
        self.padded = round_up(rows, 8)
        self.near = self.half + rows
        self.lanes = round_up(self.near, 64)
        self.first_rows = round_up(rows + self.slots + 1, 8)
        self.info_row = rows + self.slots
        self.send_rows = 2 * self.slots + 1


def dot(a, b, dims):
    return lax.dot_general(a, b, dims, preferred_element_type=F32)


def split(value):
    high = value.astype(BF16)
    low = (value - high.astype(F32)).astype(BF16)
    return high, low


def iota(shape, axis):
    return lax.broadcasted_iota(jnp.int32, shape, axis)


def fiota(shape, axis):
    return iota(shape, axis).astype(F32)


def total(value):
    return jnp.sum(jnp.sum(value, axis=0, keepdims=True), axis=1, keepdims=True)


def pick_rows(onehot, source):
    width = source.shape[1]
    high, low = split(source)
    out = dot(onehot, jnp.concatenate([high, low], axis=1), NN)
    return out[:, :width], out[:, width:]


def tile_inputs(pairs):
    high = low = None
    for onehot, source in pairs:
        h, l = pick_rows(onehot, source)
        high = h if high is None else high + h
        low = l if low is None else low + l
    return jnp.concatenate([high, low], axis=0).astype(BF16)


def place(result, acc, index, lanes):
    lane = iota(acc.shape, 1)
    return jnp.where((lane == index) | (lane == lanes + index), result, acc)


def tile_products(tiles_ref, count, inputs, lanes, group=4):
    width = inputs.shape[1]
    weights = jnp.concatenate([inputs, inputs], axis=1)
    acc = jnp.zeros((width, 2 * lanes), F32)
    for start in range(0, count, group):
        size = min(group, count - start)
        out = dot(tiles_ref[start * width : (start + size) * width, :], weights, NT)
        for inner in range(size):
            acc = place(out[inner * width : (inner + 1) * width], acc, start + inner, lanes)
    return acc


def sum_rows(select, products):
    high, low = split(products)
    return dot(
        jnp.concatenate([select, select], axis=1),
        jnp.concatenate([high, low], axis=1),
        NT,
    )


def lane_row(values):
    lane = iota((1, 128), 1)
    row = jnp.zeros((1, 128), F32)
    for index, value in enumerate(values):
        row = jnp.where(lane == index, value, row)
    return row


def push_select(z, row_meta):
    slots = z.slots * z.devices
    return (fiota((slots, 2 * z.lanes), 0) == row_meta[1:2, :]).astype(BF16)


def far_products(z, far_ref, col_meta, row_meta, source):
    onehot = (fiota((z.lanes, source.shape[0]), 1) == col_meta[:, 1:2]).astype(BF16)
    inputs = tile_inputs([(onehot, source)])
    products = tile_products(far_ref, z.half, inputs, z.lanes)
    return sum_rows(push_select(z, row_meta), products)


def prepare_kernel(
    z,
    rows_smem,
    rows_ref,
    cols_ref,
    defect_ref,
    coupling_ref,
    send_ref,
    far_ref,
    row_meta_ref,
    col_meta_ref,
    ids_ref,
    tiles,
    own,
    index,
    sems,
):
    me = lax.axis_index("blk")
    base = me * z.rows
    width = z.width
    near = jnp.int32(0)
    far = jnp.int32(0)
    for t in range(z.tiles):
        row = rows_smem[t]
        here = ((row >= base) & (row < base + z.rows)).astype(jnp.int32)
        ids_ref[near] = jnp.int32(t)
        ids_ref[z.half + 1 + far] = jnp.int32(t)
        near = near + here
        far = far + 1 - here
    copies = []
    for k in range(z.half):
        copy = pltpu.make_async_copy(
            coupling_ref.at[ids_ref[z.half + 1 + k]], tiles.at[k], sems.at[k]
        )
        copy.start()
        copies.append(copy)

    own[...] = jnp.zeros_like(own)
    own[0 : z.rows, :] = defect_ref[...]
    defect = own[...]

    count = index.shape[1]
    index[...] = jnp.full(index.shape, -1, jnp.int32)
    index[0:1, 0 : z.tiles] = rows_ref[...]
    index[1:2, 0 : z.tiles] = cols_ref[...]
    rows = index[0:1, :].astype(F32)
    cols = index[1:2, :].astype(F32)
    valid = rows >= 0
    row_owner = jnp.floor((rows + 0.5) * (1.0 / z.rows))
    col_owner = jnp.floor((cols + 0.5) * (1.0 / z.rows))
    row_local = rows - row_owner * z.rows
    col_local = cols - col_owner * z.rows
    mine = me.astype(F32)
    is_far = valid & (row_owner != mine)
    is_near = valid & (row_owner == mine)
    far_owner = jnp.where(is_far, row_owner, col_owner)
    far_local = jnp.where(is_far, row_local, col_local)
    own_local = jnp.where(is_far, col_local, row_local)
    kind = jnp.where(is_far, 1.0, jnp.where(is_near, 0.0, -1.0))
    key = jnp.where(valid, kind * z.devices + far_owner, -1.0)
    square = (count, count)
    before = iota(square, 0) < iota(square, 1)

    def ranks(value):
        wide = jnp.broadcast_to(value, square)
        same = (wide.T == wide) & before
        return jnp.sum(same.astype(F32), axis=0, keepdims=True)

    slot = ranks(key)
    position = ranks(kind)
    facts = jnp.concatenate(
        [
            far_owner,
            far_local,
            own_local + 1.0,
            slot * z.devices + far_owner + 1.0,
            slot,
            jnp.zeros((3, count), F32),
        ],
        axis=0,
    )
    facts = jnp.where(valid, facts, 0.0).astype(BF16)
    where = fiota((z.lanes, count), 0)
    near_pick = ((position == where) & is_near).astype(BF16)
    far_pick = ((position == where) & is_far).astype(BF16)
    near_rows = dot(facts, near_pick, NT)
    far_rows = dot(facts, far_pick, NT)
    near_cols = dot(near_pick, facts, NT)
    far_cols = dot(far_pick, facts, NT)

    place_row = fiota((1, z.lanes), 1) - z.half
    diag_row = (place_row >= 0) & (place_row < z.rows)
    near_target = jnp.where(diag_row, place_row, near_rows[2:3, :] - 1.0)
    far_target = far_rows[3:4, :] - 1.0
    row_meta_ref[...] = jnp.concatenate(
        [
            jnp.concatenate([near_target, near_target], axis=1),
            jnp.concatenate([far_target, far_target], axis=1),
            jnp.zeros((6, 2 * z.lanes), F32),
        ],
        axis=0,
    )
    lane = iota((z.lanes, 128), 1)
    place_col = fiota((z.lanes, 1), 0) - z.half
    diag_col = (place_col >= 0) & (place_col < z.rows)
    near_source = near_cols[:, 3:4] - 1.0
    first_source = near_cols[:, 0:1] * z.first_rows + near_cols[:, 1:2]
    first_source = jnp.where(near_source >= 0, first_source, -1.0)
    first_source = jnp.where(diag_col, mine * z.first_rows + place_col, first_source)
    near_source = jnp.where(diag_col, z.slots * z.devices + place_col, near_source)
    meta = jnp.where(lane == 0, near_source, 0.0)
    meta = jnp.where(lane == 1, far_cols[:, 2:3] - 1.0, meta)
    meta = jnp.where(lane == 2, first_source, meta)
    col_meta_ref[...] = meta

    owner = fiota((z.devices, z.lanes), 0)
    lane_f = lane.astype(F32)
    near_valid = near_cols[:, 3:4] > 0
    far_valid = far_cols[:, 3:4] > 0
    ask = jnp.where((lane_f == near_cols[:, 4:5]) & near_valid, near_cols[:, 1:2] + 1.0, 0.0)
    land = jnp.where(
        (lane_f == far_cols[:, 4:5] + z.slots) & far_valid, far_cols[:, 1:2] + 1.0, 0.0
    )
    info = dot(
        (owner == near_rows[0:1, :]).astype(BF16), ask.astype(BF16), NN
    ) + dot((owner == far_rows[0:1, :]).astype(BF16), land.astype(BF16), NN)

    send_ref[:, 0 : z.padded, :] = jnp.broadcast_to(
        defect[None, :, :], (z.devices, z.padded, width)
    )
    if z.first_rows > z.padded:
        send_ref[:, z.padded :, :] = jnp.zeros(
            (z.devices, z.first_rows - z.padded, width), F32
        )
    send_ref[:, z.info_row, :] = info

    onehot = (fiota((z.lanes, z.padded), 1) == (far_cols[:, 2:3] - 1.0)).astype(BF16)
    inputs = tile_inputs([(onehot, defect)])
    weights = jnp.concatenate([inputs, inputs], axis=1)
    acc = jnp.zeros((width, 2 * z.lanes), F32)
    for k in range(z.half):
        copies[k].wait()
        high, low = split(tiles[k])
        both = jnp.concatenate([high, low], axis=1)
        far_ref[k * width : (k + 1) * width, :] = both
        acc = place(dot(both, weights, NT), acc, k, z.lanes)
    pushes = sum_rows(push_select(z, row_meta_ref[...]), acc)
    for s in range(z.slots):
        send_ref[:, z.rows + s, :] = pushes[s * z.devices : (s + 1) * z.devices]


def gather_kernel(z, ids_ref, coupling_ref, diag_ref, near_ref, tiles, sems):
    width = z.width
    copies = []
    for k in range(z.near):
        source = coupling_ref.at[ids_ref[k]] if k < z.half else diag_ref.at[k - z.half]
        copy = pltpu.make_async_copy(source, tiles.at[k], sems.at[k])
        copy.start()
        copies.append(copy)
    for k in range(z.near):
        copies[k].wait()
        high, low = split(tiles[k])
        near_ref[k * width : (k + 1) * width, :] = jnp.concatenate([high, low], axis=1)


def own_rows(scratch, ref, z):
    scratch[...] = jnp.zeros_like(scratch)
    scratch[0 : z.rows, :] = ref[...]
    return scratch[...]


def landed(z, info, received):
    marks = []
    for s in range(z.slots):
        target = info[:, z.slots + s : z.slots + s + 1] - 1.0
        marks.append((fiota((z.devices, z.padded), 1) == target).astype(BF16))
    mark = jnp.concatenate(marks, axis=0)
    high, low = split(jnp.concatenate(received, axis=0))
    out = dot(mark, jnp.concatenate([high, low], axis=1), TN)
    return out[:, : z.width] + out[:, z.width :]


def fill_send(z, send_ref, info, far_ref, col_meta, row_meta, vector, dots):
    for s in range(z.slots):
        asked = info[:, s : s + 1] - 1.0
        onehot = (fiota((z.devices, z.padded), 1) == asked).astype(BF16)
        high, low = pick_rows(onehot, vector)
        send_ref[:, s, :] = high + low
    send_ref[:, 2 * z.slots, :] = jnp.broadcast_to(lane_row(dots), (z.devices, 128))
    pushes = far_products(z, far_ref, col_meta, row_meta, vector)
    for s in range(z.slots):
        send_ref[:, z.slots + s, :] = pushes[s * z.devices : (s + 1) * z.devices]


def near_select(z, row_meta):
    return (fiota((z.padded, 2 * z.lanes), 0) == row_meta[0:1, :]).astype(BF16)


def first_kernel(
    z,
    received_ref,
    near_ref,
    far_ref,
    defect_ref,
    mass_ref,
    row_meta_ref,
    col_meta_ref,
    send_ref,
    state_ref,
    info_ref,
    scalar_ref,
    own,
    own_mass,
):
    defect = own_rows(own, defect_ref, z)
    mass = own_rows(own_mass, mass_ref, z)
    row_meta = row_meta_ref[...]
    col_meta = col_meta_ref[...]
    everything = received_ref[...]
    real = iota(everything.shape, 1) < z.rows
    squares = jnp.sum(jnp.where(real, everything * everything, 0.0), axis=0)
    beta_square = total(squares)
    scale = -1.0 / jnp.sqrt(beta_square)
    flat = everything.reshape(z.devices * z.first_rows, z.width)
    onehot = (fiota((z.lanes, flat.shape[0]), 1) == col_meta[:, 2:3]).astype(BF16)
    inputs = tile_inputs([(onehot, flat)])
    products = tile_products(near_ref, z.near, inputs, z.lanes)
    image = mass * defect + sum_rows(near_select(z, row_meta), products)
    info = received_ref[:, z.info_row, :]
    info_ref[...] = info
    image = image + landed(
        z, info, [received_ref[:, z.rows + s, :] for s in range(z.slots)]
    )
    v0 = defect * scale
    w0 = image * scale
    dots = [total(w0 * v0), total(w0 * w0)]
    state_ref[0] = v0
    state_ref[1] = w0
    scalar_ref[...] = jnp.broadcast_to(jnp.sqrt(beta_square), scalar_ref.shape)
    fill_send(z, send_ref, info, far_ref, col_meta, row_meta, w0, dots)


def apply_received(z, received_ref, near_ref, info, mass, row_meta, col_meta, vector):
    sources = [received_ref[:, s, :] for s in range(z.slots)] + [vector]
    source = jnp.concatenate(sources, axis=0)
    onehot = (fiota((z.lanes, source.shape[0]), 1) == col_meta[:, 0:1]).astype(BF16)
    inputs = tile_inputs([(onehot, source)])
    products = tile_products(near_ref, z.near, inputs, z.lanes)
    image = mass * vector + sum_rows(near_select(z, row_meta), products)
    return image + landed(
        z, info, [received_ref[:, z.slots + s, :] for s in range(z.slots)]
    )


def summed_dots(z, received_ref, row):
    sums = jnp.sum(received_ref[:, row, :], axis=0, keepdims=True)
    return lambda index: sums[:, index : index + 1]


def second_kernel(
    z,
    received_ref,
    near_ref,
    far_ref,
    mass_ref,
    row_meta_ref,
    col_meta_ref,
    state_in,
    info_ref,
    scalar_in,
    send_ref,
    state_ref,
    scalar_ref,
    own_mass,
):
    mass = own_rows(own_mass, mass_ref, z)
    row_meta = row_meta_ref[...]
    col_meta = col_meta_ref[...]
    info = info_ref[...]
    v0 = state_in[0]
    w0 = state_in[1]
    image = apply_received(
        z, received_ref, near_ref, info, mass, row_meta, col_meta, w0
    )
    get = summed_dots(z, received_ref, 2 * z.slots)
    h00, g00 = get(0), get(1)
    inverse = lax.rsqrt(jnp.maximum(g00 - h00 * h00, FLOOR * g00))
    v1 = (w0 - h00 * v0) * inverse
    w1 = (image - h00 * w0) * inverse
    dots = [total(w1 * v0), total(w1 * v1), total(w1 * w1), total(w1 * w0)]
    state_ref[0] = v0
    state_ref[1] = v1
    state_ref[2] = w0
    state_ref[3] = w1
    scalar_ref[...] = jnp.broadcast_to(
        lane_row([scalar_in[0:1, 0:1], h00, g00]), scalar_ref.shape
    )
    fill_send(z, send_ref, info, far_ref, col_meta, row_meta, w1, dots)


def third_kernel(
    z,
    received_ref,
    near_ref,
    mass_ref,
    row_meta_ref,
    col_meta_ref,
    state_in,
    info_ref,
    scalar_in,
    send_ref,
    state_ref,
    scalar_ref,
    own_mass,
):
    mass = own_rows(own_mass, mass_ref, z)
    v0, v1, w0, w1 = state_in[0], state_in[1], state_in[2], state_in[3]
    image = apply_received(
        z,
        received_ref,
        near_ref,
        info_ref[...],
        mass,
        row_meta_ref[...],
        col_meta_ref[...],
        w1,
    )
    get = summed_dots(z, received_ref, 2 * z.slots)
    h01, h11, g11, g01 = get(0), get(1), get(2), get(3)
    inverse = lax.rsqrt(jnp.maximum(g11 - h01 * h01 - h11 * h11, FLOOR * g11))
    v2 = (w1 - h01 * v0 - h11 * v1) * inverse
    w2 = (image - h01 * w0 - h11 * w1) * inverse
    dots = [total(w2 * v0), total(w2 * w0), total(w2 * w1), total(w2 * w2)]
    state_ref[0] = v0
    state_ref[1] = v1
    state_ref[2] = v2
    old = scalar_in[0:1, :]
    scalar_ref[...] = jnp.broadcast_to(
        lane_row([old[:, 0:1], old[:, 1:2], old[:, 2:3], h01, g01, g11]),
        scalar_ref.shape,
    )
    send_ref[:, 0, :] = jnp.broadcast_to(lane_row(dots), (z.devices, 128))


def last_kernel(z, received_ref, state_in, scalar_in, out_ref):
    get = summed_dots(z, received_ref, 0)
    d, g02, g12, g22 = get(0), get(1), get(2), get(3)
    old = scalar_in[0:1, :]
    beta, h00, g00 = old[:, 0:1], old[:, 1:2], old[:, 2:3]
    h01, g01, g11 = old[:, 3:4], old[:, 4:5], old[:, 5:6]
    b0, b1, b2 = beta * h00, beta * h01, beta * d
    l00 = jnp.sqrt(g00)
    l10 = g01 / l00
    l20 = g02 / l00
    l11 = jnp.sqrt(g11 - l10 * l10)
    l21 = (g12 - l20 * l10) / l11
    l22 = jnp.sqrt(g22 - l20 * l20 - l21 * l21)
    f0 = b0 / l00
    f1 = (b1 - l10 * f0) / l11
    f2 = (b2 - l20 * f0 - l21 * f1) / l22
    y2 = f2 / l22
    y1 = (f1 - l21 * y2) / l11
    y0 = (f0 - l10 * y1 - l20 * y2) / l00
    update = y0 * state_in[0] + y1 * state_in[1] + y2 * state_in[2]
    out_ref[...] = update[0 : z.rows, :]


def on_device(defect, mass, block_diag, coupling, tile_rows, tile_cols):
    z = Sizes(lax.axis_size("blk"), defect.shape[0], defect.shape[1], tile_rows.shape[0])
    width = z.width
    vmem = pl.BlockSpec(memory_space=pltpu.VMEM)
    smem = pl.BlockSpec(memory_space=pltpu.SMEM)
    anywhere = pl.BlockSpec(memory_space=pl.ANY)

    def shape(*dims, dtype=F32):
        return jax.ShapeDtypeStruct(dims, dtype)

    def call(kernel, name, ins, outs, scratch, args, limit):
        return pl.pallas_call(
            functools.partial(kernel, z),
            out_shape=[item[0] for item in outs],
            in_specs=ins,
            out_specs=[item[1] for item in outs],
            scratch_shapes=scratch,
            name=name,
            compiler_params=pltpu.CompilerParams(vmem_limit_bytes=limit * MIB),
        )(*args)

    rows_2d = tile_rows.reshape(1, z.tiles)
    cols_2d = tile_cols.reshape(1, z.tiles)
    index_width = round_up(z.tiles, 128)
    tile_bytes = -(-z.near * width * width * 4 // MIB)
    send, far, row_meta, col_meta, ids = call(
        prepare_kernel,
        "prepare",
        [smem, vmem, vmem, vmem, anywhere],
        [
            (shape(z.devices, z.first_rows, width), vmem),
            (shape(z.half * width, 2 * width, dtype=BF16), vmem),
            (shape(8, 2 * z.lanes), vmem),
            (shape(z.lanes, 128), vmem),
            (shape(2 * z.half + 2, dtype=jnp.int32), smem),
        ],
        [
            pltpu.VMEM((z.half, width, width), F32),
            pltpu.VMEM((z.padded, width), F32),
            pltpu.VMEM((8, index_width), jnp.int32),
            pltpu.SemaphoreType.DMA((z.half,)),
        ],
        (tile_rows, rows_2d, cols_2d, defect, coupling),
        2 * tile_bytes + 8,
    )
    received = lax.all_to_all(send, "blk", split_axis=0, concat_axis=0, tiled=True)
    (near,) = call(
        gather_kernel,
        "gather",
        [smem, anywhere, anywhere],
        [(shape(z.near * width, 2 * width, dtype=BF16), vmem)],
        [
            pltpu.VMEM((z.near, width, width), F32),
            pltpu.SemaphoreType.DMA((z.near,)),
        ],
        (ids, coupling, block_diag),
        2 * tile_bytes + 4,
    )
    send, state, info, scalars = call(
        first_kernel,
        "first",
        [vmem] * 7,
        [
            (shape(z.devices, z.send_rows, width), vmem),
            (shape(2, z.padded, width), vmem),
            (shape(z.devices, 128), vmem),
            (shape(8, 128), vmem),
        ],
        [pltpu.VMEM((z.padded, width), F32)] * 2,
        (received, near, far, defect, mass, row_meta, col_meta),
        2 * tile_bytes + 8,
    )
    received = lax.all_to_all(send, "blk", split_axis=0, concat_axis=0, tiled=True)
    send, state, scalars = call(
        second_kernel,
        "second",
        [vmem] * 9,
        [
            (shape(z.devices, z.send_rows, width), vmem),
            (shape(4, z.padded, width), vmem),
            (shape(8, 128), vmem),
        ],
        [pltpu.VMEM((z.padded, width), F32)],
        (received, near, far, mass, row_meta, col_meta, state, info, scalars),
        2 * tile_bytes + 8,
    )
    received = lax.all_to_all(send, "blk", split_axis=0, concat_axis=0, tiled=True)
    send, state, scalars = call(
        third_kernel,
        "third",
        [vmem] * 8,
        [
            (shape(z.devices, 1, width), vmem),
            (shape(3, z.padded, width), vmem),
            (shape(8, 128), vmem),
        ],
        [pltpu.VMEM((z.padded, width), F32)],
        (received, near, mass, row_meta, col_meta, state, info, scalars),
        2 * tile_bytes + 8,
    )
    received = lax.all_to_all(send, "blk", split_axis=0, concat_axis=0, tiled=True)
    (update,) = call(
        last_kernel,
        "last",
        [vmem] * 3,
        [(shape(z.rows, width), vmem)],
        [],
        (received, state, scalars),
        4,
    )
    return update


def solution(mesh):
    in_specs = (
        P("blk", None),
        P("blk", None),
        P("blk", None, None),
        P("blk", None, None),
        P("blk"),
        P("blk"),
    )
    return jax.shard_map(
        on_device, mesh=mesh, in_specs=in_specs, out_specs=P("blk", None), check_vma=False
    )
```

time: 496 us -> 84.9 us (0.17)
  blocking collectives: 277 us -> 32.8 us
  local copies, waits for them, and re-layouts: 64.7 us -> 13.4 us
  matrix products: 42.4 us -> 0 us
  waiting for transfers between devices: 40.1 us -> 0.01 us
  Pallas kernels: 0 us -> 31 us
  other arithmetic: 25.1 us -> 0 us
  starting transfers between devices: 32.3 us -> 7.33 us
  between operations: 12.6 us -> 0.1 us
    psum x7 -> x0, blocking collectives: 277 us -> none  [the longest x3 121 us: on_device(): norm = jnp.sqrt(lax.psum(jnp.sum(image * image), 'blk'))]
    scatter x11 -> x0, local copies, waits for them, and re-layouts: 47.7 us -> none  [the longest x3 34 us: on_device(): outgoing = jnp.zeros((devices, slots, width), jnp.float32).at[push_lane,...]
    dot_general x13 -> x0, matrix products: 42.4 us -> none  [the longest x3 35.5 us: tile_products(): jnp.einsum('tij,tj->ti', coupling, inputs, precision=lax.Precision.HIGHEST)]
    all_to_all x8 -> x1, waiting for transfers between devices: 40.1 us -> 0.01 us  [on_device(): lax.all_to_all(send, 'blk', split_axis=0, concat_axis=0, tiled=True)]
    all_to_all x0 -> x3, blocking collectives: none -> 32.8 us  [on_device(): lax.all_to_all(send, 'blk', split_axis=0, concat_axis=0, tiled=True)]
    pallas_call x0 -> x6, Pallas kernels: none -> 31 us  [call(): pl.pallas_call(functools.partial(kernel, z), out_shape=[item[0] for item...]
    all_to_all x8 -> x1, starting transfers between devices: 32.3 us -> 7.33 us  [on_device(): lax.all_to_all(send, 'blk', split_axis=0, concat_axis=0, tiled=True)]
    unnamed x6 -> x24, local copies, waits for them, and re-layouts: 0.01 us -> 13.4 us
  transfers between devices with their start and end apart: 8 -> 1, of which waited for: 7 -> 0; matrix products, arithmetic and copies ran while one was open for 4% -> 0% of each run, Pallas kernels for 0% -> 8%
where the time goes in v1:
time: 84.9 us; the launch traced here: 84.5 us
  blocking collectives  32.8 us (39%)
  Pallas kernels  31 us (37%)
  local copies, waits for them, and re-layouts  13.4 us (16%)
  starting transfers between devices  7.33 us (9%)
    all_to_all x3, blocking collectives, on_device(): lax.all_to_all(send, 'blk', split_axis=0, concat_axis=0, tiled=True)  32.8 us
    pallas_call x6, Pallas kernels, call(): pl.pallas_call(functools.partial(kernel, z), out_shape=[item[0] for item...  31 us
    unnamed x24, local copies, waits for them, and re-layouts  13.4 us
    all_to_all x1, starting transfers between devices, on_device(): lax.all_to_all(send, 'blk', split_axis=0, concat_axis=0, tiled=True)  7.33 us
  transfers between devices with their start and end apart: 1, of which 0 were waited for; matrix products, arithmetic and copies ran while one was open for 0% of the time, Pallas kernels for 8%

profile of v1, /device:TPU:0, one launch (start us, length us, event | category | flops | bytes accessed | tf_op | source)
XLA Modules:
  0.0 84.5 jit_solution(13995601551551422346)
XLA Ops:
  0.0 0.0 copy-start.3
  0.0 2.8 %copy-done.3 = f32[96,128,128]{2,1,0:T(8,128)S(1)} copy-done((f32[96,128,128]{2,1,0:T(8,128)S(1)}, f32[96,128,128]{2,1,0:T(8,128)}, u32[]{:S(2)}) %copy-start.3) | copy-done | bytes 6291480
  2.8 0.0 copy-start.8
  2.8 0.7 copy-done.8
  3.5 0.0 copy-start.10
  3.5 0.7 copy-done.10
  4.1 0.0 copy-start.11
  4.1 0.7 copy-done.11
  4.8 15.2 %prepare.1 = (f32[32,16,128]{2,1,0:T(8,128)S(1)}, bf16[6144,256]{1,0:T(8,128)(2,1)S(1)}, f32[8,128]{1,0:T(8,128)S(1)}, f32[64,128]{1,0:T(8,128)S(1)}, s32[98]{0:T(128)S(1)}) custom-call(s32[96]{0:T(128)S(1)} %copy-done.10, s32[1,96]{1,0:T(1,128)S(1)} %bitcast.2, s32[1,96]{1,0:T(1,128)S(1)} %bitcast.3, f32[12,128]{1,0:T(8,128)S(1)} %copy-done.8, ...), custom_call_target="tpu_custom_call" | custom-call | tf_op jit(solution)/shard_map/prepare/pallas_call | solution.py:501
  20.0 0.0 copy-start.6
  20.0 0.7 copy-done.6
  20.7 7.3 %all-to-all-start = ((f32[32,16,128]{2,1,0:T(8,128)}), f32[32,16,128]{2,1,0:T(8,128)S(1)}, u32[]{:S(2)}, u32[]{:S(2)}) async-start(f32[32,16,128]{2,1,0:T(8,128)} %copy-done.6), calls=%async_computation | async-start | bytes 524288 | tf_op jit(solution)/shard_map/all_to_all | solution.py:535
  28.1 0.0 copy-start.4
  28.1 2.8 %copy-done.4 = f32[96,128,128]{2,1,0:T(8,128)S(1)} copy-done((f32[96,128,128]{2,1,0:T(8,128)S(1)}, f32[96,128,128]{2,1,0:T(8,128)}, u32[]{:S(2)}) %copy-start.4) | copy-done | bytes 6291480
  30.9 0.0 copy-start.5
  30.9 1.1 %copy-done.5 = f32[12,128,128]{2,1,0:T(8,128)S(1)} copy-done((f32[12,128,128]{2,1,0:T(8,128)S(1)}, f32[12,128,128]{2,1,0:T(8,128)}, u32[]{:S(2)}) %copy-start.5) | copy-done | bytes 786456
  32.0 0.0 copy-start.7
  32.0 0.0 copy-start.9
  32.0 7.0 %gather.1.near_ref = bf16[7680,256]{1,0:T(8,128)(2,1)S(1)} custom-call(s32[98]{0:T(128)S(1)} %get-tuple-element.21.ids_ref, f32[96,128,128]{2,1,0:T(8,128)S(1)} %copy-done.4, f32[12,128,128]{2,1,0:T(8,128)S(1)} %copy-done.5), custom_call_target="tpu_custom_call" | custom-call | tf_op jit(solution)/shard_map/gather/pallas_call | solution.py:501
  39.0 0.0 copy-start
  39.0 1.8 %copy-done = bf16[7680,256]{1,0:T(8,128)(2,1)} copy-done((bf16[7680,256]{1,0:T(8,128)(2,1)}, bf16[7680,256]{1,0:T(8,128)(2,1)S(1)}, u32[]{:S(2)}) %copy-start) | copy-done | bytes 3932184
  40.9 0.0 all-to-all-done.received_ref
  40.9 0.0 copy-done.7
  40.9 0.0 copy-done.9
  40.9 0.0 copy-start.1
  40.9 2.1 %copy-done.1 = bf16[7680,256]{1,0:T(8,128)(2,1)S(1)} copy-done((bf16[7680,256]{1,0:T(8,128)(2,1)S(1)}, bf16[7680,256]{1,0:T(8,128)(2,1)}, u32[]{:S(2)}) %copy-start.1) | copy-done | bytes 3932184
  43.0 0.0 copy-start.2
  43.0 2.9 %first.1 = (f32[32,5,128]{2,1,0:T(8,128)S(1)}, f32[2,16,128]{2,1,0:T(8,128)S(1)}, f32[32,128]{1,0:T(8,128)S(1)}, f32[8,128]{1,0:T(8,128)S(1)}) custom-call(f32[32,16,128]{2,1,0:T(8,128)S(1)} %all-to-all-done.received_ref, bf16[7680,256]{1,0:T(8,128)(2,1)S(1)} %copy-done.1, bf16[6144,256]{1,0:T(8,128)(2,1)S(1)} %get-tuple-element.22.far_ref, ...), custom_call_target="tpu_custom_call" | custom-call | tf_op jit(solution)/shard_map/first/pallas_call | solution.py:501
  45.9 13.8 %all_to_all.20.received_ref = f32[32,5,128]{2,1,0:T(8,128)S(1)} all-to-all(f32[32,5,128]{2,1,0:T(8,128)S(1)} %get-tuple-element.25), channel_id=1, replica_groups=mesh['blk'=32] {'blk'}, dimensions={0} | all-to-all | bytes 163840 | tf_op jit(solution)/shard_map/all_to_all | solution.py:562
  59.7 0.0 copy-done.2
  59.7 2.9 %second.1 = (f32[32,5,128]{2,1,0:T(8,128)S(1)}, f32[4,16,128]{2,1,0:T(8,128)S(1)}, f32[8,128]{1,0:T(8,128)S(1)}) custom-call(f32[32,5,128]{2,1,0:T(8,128)S(1)} %all_to_all.20.received_ref, bf16[7680,256]{1,0:T(8,128)(2,1)S(1)} %copy-done.2, bf16[6144,256]{1,0:T(8,128)(2,1)S(1)} %get-tuple-element.22.far_ref, f32[12,128]{1,0:T(8,128)S(1)} %copy-done.7, ...), custom_call_target="tpu_custom_call" | custom-call | tf_op jit(solution)/shard_map/second/pallas_call | solution.py:501
  62.6 10.0 %all_to_all.21.received_ref = f32[32,5,128]{2,1,0:T(8,128)S(1)} all-to-all(f32[32,5,128]{2,1,0:T(8,128)S(1)} %get-tuple-element.29), channel_id=1, replica_groups=mesh['blk'=32] {'blk'}, dimensions={0} | all-to-all | bytes 163840 | tf_op jit(solution)/shard_map/all_to_all | solution.py:576
  72.6 1.7 %third.1 = (f32[32,1,128]{2,1,0:T(1,128)S(1)}, f32[3,16,128]{2,1,0:T(8,128)S(1)}, f32[8,128]{1,0:T(8,128)S(1)}) custom-call(f32[32,5,128]{2,1,0:T(8,128)S(1)} %all_to_all.21.received_ref, bf16[7680,256]{1,0:T(8,128)(2,1)S(1)} %copy-done.2, f32[12,128]{1,0:T(8,128)S(1)} %copy-done.7, f32[8,128]{1,0:T(8,128)S(1)} %get-tuple-element.23.row_meta_ref, ...), custom_call_target="tpu_custom_call" | custom-call | tf_op jit(solution)/shard_map/third/pallas_call | solution.py:501
  74.3 8.9 %all_to_all.22.received_ref = f32[32,1,128]{2,1,0:T(1,128)S(1)} all-to-all(f32[32,1,128]{2,1,0:T(1,128)S(1)} %get-tuple-element.32), channel_id=1, replica_groups=mesh['blk'=32] {'blk'}, dimensions={0} | all-to-all | bytes 32768 | tf_op jit(solution)/shard_map/all_to_all | solution.py:590
  83.2 1.3 %last.1 = f32[12,128]{1,0:T(8,128)} custom-call(f32[32,1,128]{2,1,0:T(1,128)S(1)} %all_to_all.22.received_ref, f32[3,16,128]{2,1,0:T(8,128)S(1)} %get-tuple-element.33.state_in, f32[8,128]{1,0:T(8,128)S(1)} %get-tuple-element.34.scalar_in), custom_call_target="tpu_custom_call" | custom-call | tf_op jit(solution)/shard_map/last/pallas_call | solution.py:501
Async XLA Ops:
  0.0 2.8 %copy-start.3 = (f32[96,128,128]{2,1,0:T(8,128)S(1)}, f32[96,128,128]{2,1,0:T(8,128)}, u32[]{:S(2)}) copy-start(f32[96,128,128]{2,1,0:T(8,128)} %coupling_ref.3) | copy-start | bytes 18874372
  2.8 0.7 copy-start.8
  3.5 0.7 copy-start.10
  4.1 0.7 copy-start.11
  20.0 0.7 copy-start.6
  20.7 20.1 %all-to-all-start = ((f32[32,16,128]{2,1,0:T(8,128)}), f32[32,16,128]{2,1,0:T(8,128)S(1)}, u32[]{:S(2)}, u32[]{:S(2)}) async-start(f32[32,16,128]{2,1,0:T(8,128)} %copy-done.6), calls=%async_computation | async-start | bytes 524288 | tf_op jit(solution)/shard_map/all_to_all | solution.py:535
  28.1 2.8 %copy-start.4 = (f32[96,128,128]{2,1,0:T(8,128)S(1)}, f32[96,128,128]{2,1,0:T(8,128)}, u32[]{:S(2)}) copy-start(f32[96,128,128]{2,1,0:T(8,128)} %coupling_ref.3) | copy-start | bytes 18874372
  30.9 1.1 %copy-start.5 = (f32[12,128,128]{2,1,0:T(8,128)S(1)}, f32[12,128,128]{2,1,0:T(8,128)}, u32[]{:S(2)}) copy-start(f32[12,128,128]{2,1,0:T(8,128)} %diag_ref.1) | copy-start | bytes 2359300
  32.0 8.9 %copy-start.7 = (f32[12,128]{1,0:T(8,128)S(1)}, f32[12,128]{1,0:T(8,128)}, u32[]{:S(2)}) copy-start(f32[12,128]{1,0:T(8,128)} %mass_ref.5) | copy-start | bytes 18436
  32.0 8.9 %copy-start.9 = (f32[12,128]{1,0:T(8,128)S(1)}, f32[12,128]{1,0:T(8,128)}, u32[]{:S(2)}) copy-start(f32[12,128]{1,0:T(8,128)} %defect_ref.3) | copy-start | bytes 18436
  39.0 1.9 %copy-start = (bf16[7680,256]{1,0:T(8,128)(2,1)}, bf16[7680,256]{1,0:T(8,128)(2,1)S(1)}, u32[]{:S(2)}) copy-start(bf16[7680,256]{1,0:T(8,128)(2,1)S(1)} %gather.1.near_ref) | copy-start | bytes 11796484
  40.9 2.1 %copy-start.1 = (bf16[7680,256]{1,0:T(8,128)(2,1)S(1)}, bf16[7680,256]{1,0:T(8,128)(2,1)}, u32[]{:S(2)}) copy-start(bf16[7680,256]{1,0:T(8,128)(2,1)} %copy-done) | copy-start | bytes 11796484
  43.0 16.8 %copy-start.2 = (bf16[7680,256]{1,0:T(8,128)(2,1)S(1)}, bf16[7680,256]{1,0:T(8,128)(2,1)}, u32[]{:S(2)}) copy-start(bf16[7680,256]{1,0:T(8,128)(2,1)} %copy-done) | copy-start | bytes 11796484

commit v2 on v1

--- a/solution.py
+++ b/solution.py
@@ -14,6 +14,7 @@
 TN = (((0,), (0,)), ((), ()))
 FLOOR = 2.0**-22
 MIB = 1 << 20
+GROUP = 12
 
 
 def round_up(value, step):
@@ -122,24 +123,45 @@
 
 def prepare_kernel(
     z,
-    rows_smem,
-    rows_ref,
-    cols_ref,
-    defect_ref,
-    coupling_ref,
+    rows_hbm,
+    rows_2d_hbm,
+    cols_2d_hbm,
+    defect_hbm,
+    coupling_hbm,
     send_ref,
     far_ref,
     row_meta_ref,
     col_meta_ref,
     ids_ref,
+    rows_smem,
+    rows_ref,
+    cols_ref,
+    defect_ref,
     tiles,
     own,
     index,
+    small_sems,
     sems,
 ):
     me = lax.axis_index("blk")
     base = me * z.rows
     width = z.width
+    small = [
+        pltpu.make_async_copy(source, target, small_sems.at[i])
+        for i, (source, target) in enumerate(
+            [
+                (rows_hbm, rows_smem),
+                (rows_2d_hbm, rows_ref),
+                (cols_2d_hbm, cols_ref),
+                (defect_hbm, defect_ref),
+            ]
+        )
+    ]
+    for copy in small:
+        copy.start()
+    own[...] = jnp.zeros_like(own)
+    index[...] = jnp.full(index.shape, -1, jnp.int32)
+    small[0].wait()
     near = jnp.int32(0)
     far = jnp.int32(0)
     for t in range(z.tiles):
@@ -152,17 +174,17 @@
     copies = []
     for k in range(z.half):
         copy = pltpu.make_async_copy(
-            coupling_ref.at[ids_ref[z.half + 1 + k]], tiles.at[k], sems.at[k]
+            coupling_hbm.at[ids_ref[z.half + 1 + k]], tiles.at[k], sems.at[k]
         )
         copy.start()
         copies.append(copy)
-
-    own[...] = jnp.zeros_like(own)
+    for copy in small[1:]:
+        copy.wait()
+
     own[0 : z.rows, :] = defect_ref[...]
     defect = own[...]
 
     count = index.shape[1]
-    index[...] = jnp.full(index.shape, -1, jnp.int32)
     index[0:1, 0 : z.tiles] = rows_ref[...]
     index[1:2, 0 : z.tiles] = cols_ref[...]
     rows = index[0:1, :].astype(F32)
@@ -214,7 +236,7 @@
     diag_row = (place_row >= 0) & (place_row < z.rows)
     near_target = jnp.where(diag_row, place_row, near_rows[2:3, :] - 1.0)
     far_target = far_rows[3:4, :] - 1.0
-    row_meta_ref[...] = jnp.concatenate(
+    row_meta = jnp.concatenate(
         [
             jnp.concatenate([near_target, near_target], axis=1),
             jnp.concatenate([far_target, far_target], axis=1),
@@ -222,6 +244,7 @@
         ],
         axis=0,
     )
+    row_meta_ref[...] = row_meta
     lane = iota((z.lanes, 128), 1)
     place_col = fiota((z.lanes, 1), 0) - z.half
     diag_col = (place_col >= 0) & (place_col < z.rows)
@@ -260,29 +283,25 @@
     inputs = tile_inputs([(onehot, defect)])
     weights = jnp.concatenate([inputs, inputs], axis=1)
     acc = jnp.zeros((width, 2 * z.lanes), F32)
-    for k in range(z.half):
-        copies[k].wait()
-        high, low = split(tiles[k])
-        both = jnp.concatenate([high, low], axis=1)
-        far_ref[k * width : (k + 1) * width, :] = both
-        acc = place(dot(both, weights, NT), acc, k, z.lanes)
-    pushes = sum_rows(push_select(z, row_meta_ref[...]), acc)
+    for start in range(0, z.half, GROUP):
+        group = range(start, min(start + GROUP, z.half))
+        for k in group:
+            copies[k].wait()
+        for k in group:
+            far_ref[k * width : (k + 1) * width, :] = both_pieces(tiles[k])
+        out = dot(
+            far_ref[start * width : (group[-1] + 1) * width, :], weights, NT
+        )
+        for k in group:
+            acc = place(out[(k - start) * width : (k - start + 1) * width], acc, k, z.lanes)
+    pushes = sum_rows(push_select(z, row_meta), acc)
     for s in range(z.slots):
         send_ref[:, z.rows + s, :] = pushes[s * z.devices : (s + 1) * z.devices]
 
 
-def gather_kernel(z, ids_ref, coupling_ref, diag_ref, near_ref, tiles, sems):
-    width = z.width
-    copies = []
-    for k in range(z.near):
-        source = coupling_ref.at[ids_ref[k]] if k < z.half else diag_ref.at[k - z.half]
-        copy = pltpu.make_async_copy(source, tiles.at[k], sems.at[k])
-        copy.start()
-        copies.append(copy)
-    for k in range(z.near):
-        copies[k].wait()
-        high, low = split(tiles[k])
-        near_ref[k * width : (k + 1) * width, :] = jnp.concatenate([high, low], axis=1)
+def both_pieces(tile):
+    high, low = split(tile)
+    return jnp.concatenate([high, low], axis=1)
 
 
 def own_rows(scratch, ref, z):
@@ -321,19 +340,47 @@
 def first_kernel(
     z,
     received_ref,
-    near_ref,
     far_ref,
-    defect_ref,
-    mass_ref,
     row_meta_ref,
     col_meta_ref,
+    ids_hbm,
+    defect_hbm,
+    mass_hbm,
+    coupling_hbm,
+    diag_hbm,
     send_ref,
     state_ref,
     info_ref,
     scalar_ref,
+    near_ref,
+    mass_out_ref,
+    ids_ref,
+    defect_ref,
+    mass_ref,
+    tiles,
+    diag,
     own,
     own_mass,
+    small_sems,
+    sems,
 ):
+    width = z.width
+    ids_copy = pltpu.make_async_copy(ids_hbm, ids_ref, small_sems.at[0])
+    diag_copy = pltpu.make_async_copy(diag_hbm, diag, small_sems.at[1])
+    defect_copy = pltpu.make_async_copy(defect_hbm, defect_ref, small_sems.at[2])
+    mass_copy = pltpu.make_async_copy(mass_hbm, mass_ref, small_sems.at[3])
+    for copy in (ids_copy, defect_copy, mass_copy, diag_copy):
+        copy.start()
+    ids_copy.wait()
+    copies = []
+    for k in range(z.half):
+        copy = pltpu.make_async_copy(
+            coupling_hbm.at[ids_ref[k]], tiles.at[k], sems.at[k]
+        )
+        copy.start()
+        copies.append(copy)
+    defect_copy.wait()
+    mass_copy.wait()
     defect = own_rows(own, defect_ref, z)
     mass = own_rows(own_mass, mass_ref, z)
     row_meta = row_meta_ref[...]
@@ -346,7 +393,24 @@
     flat = everything.reshape(z.devices * z.first_rows, z.width)
     onehot = (fiota((z.lanes, flat.shape[0]), 1) == col_meta[:, 2:3]).astype(BF16)
     inputs = tile_inputs([(onehot, flat)])
-    products = tile_products(near_ref, z.near, inputs, z.lanes)
+    weights = jnp.concatenate([inputs, inputs], axis=1)
+    products = jnp.zeros((width, 2 * z.lanes), F32)
+    diag_copy.wait()
+    groups = [range(z.half, z.near)]
+    groups += [
+        range(start, min(start + GROUP, z.half)) for start in range(0, z.half, GROUP)
+    ]
+    for group in groups:
+        if group[0] < z.half:
+            for k in group:
+                copies[k].wait()
+        for k in group:
+            tile = tiles[k] if k < z.half else diag[k - z.half]
+            near_ref[k * width : (k + 1) * width, :] = both_pieces(tile)
+        low, high = group[0] * width, (group[-1] + 1) * width
+        out = dot(near_ref[low:high, :], weights, NT)
+        for i, k in enumerate(group):
+            products = place(out[i * width : (i + 1) * width], products, k, z.lanes)
     image = mass * defect + sum_rows(near_select(z, row_meta), products)
     info = received_ref[:, z.info_row, :]
     info_ref[...] = info
@@ -358,6 +422,7 @@
     dots = [total(w0 * v0), total(w0 * w0)]
     state_ref[0] = v0
     state_ref[1] = w0
+    mass_out_ref[...] = mass
     scalar_ref[...] = jnp.broadcast_to(jnp.sqrt(beta_square), scalar_ref.shape)
     fill_send(z, send_ref, info, far_ref, col_meta, row_meta, w0, dots)
 
@@ -393,9 +458,8 @@
     send_ref,
     state_ref,
     scalar_ref,
-    own_mass,
 ):
-    mass = own_rows(own_mass, mass_ref, z)
+    mass = mass_ref[...]
     row_meta = row_meta_ref[...]
     col_meta = col_meta_ref[...]
     info = info_ref[...]
@@ -433,9 +497,8 @@
     send_ref,
     state_ref,
     scalar_ref,
-    own_mass,
 ):
-    mass = own_rows(own_mass, mass_ref, z)
+    mass = mass_ref[...]
     v0, v1, w0, w1 = state_in[0], state_in[1], state_in[2], state_in[3]
     image = apply_received(
         z,
@@ -492,7 +555,7 @@
     width = z.width
     vmem = pl.BlockSpec(memory_space=pltpu.VMEM)
     smem = pl.BlockSpec(memory_space=pltpu.SMEM)
-    anywhere = pl.BlockSpec(memory_space=pl.ANY)
+    hbm = pl.BlockSpec(memory_space=pltpu.HBM)
 
     def shape(*dims, dtype=F32):
         return jax.ShapeDtypeStruct(dims, dtype)
@@ -508,14 +571,20 @@
             compiler_params=pltpu.CompilerParams(vmem_limit_bytes=limit * MIB),
         )(*args)
 
-    rows_2d = tile_rows.reshape(1, z.tiles)
-    cols_2d = tile_cols.reshape(1, z.tiles)
+    def in_hbm(value):
+        return pltpu.with_memory_space_constraint(value, pltpu.HBM)
+
+    rows_2d = in_hbm(tile_rows.reshape(1, z.tiles))
+    cols_2d = in_hbm(tile_cols.reshape(1, z.tiles))
+    tile_rows, coupling, block_diag, defect, mass = map(
+        in_hbm, (tile_rows, coupling, block_diag, defect, mass)
+    )
     index_width = round_up(z.tiles, 128)
-    tile_bytes = -(-z.near * width * width * 4 // MIB)
+    tile = width * width * 4
     send, far, row_meta, col_meta, ids = call(
         prepare_kernel,
         "prepare",
-        [smem, vmem, vmem, vmem, anywhere],
+        [hbm] * 5,
         [
             (shape(z.devices, z.first_rows, width), vmem),
             (shape(z.half * width, 2 * width, dtype=BF16), vmem),
@@ -524,40 +593,45 @@
             (shape(2 * z.half + 2, dtype=jnp.int32), smem),
         ],
         [
+            pltpu.SMEM((z.tiles,), jnp.int32),
+            pltpu.VMEM((1, z.tiles), jnp.int32),
+            pltpu.VMEM((1, z.tiles), jnp.int32),
+            pltpu.VMEM((z.rows, width), F32),
             pltpu.VMEM((z.half, width, width), F32),
             pltpu.VMEM((z.padded, width), F32),
             pltpu.VMEM((8, index_width), jnp.int32),
+            pltpu.SemaphoreType.DMA((4,)),
             pltpu.SemaphoreType.DMA((z.half,)),
         ],
         (tile_rows, rows_2d, cols_2d, defect, coupling),
-        2 * tile_bytes + 8,
+        2 * z.half * tile // MIB + 4,
     )
     received = lax.all_to_all(send, "blk", split_axis=0, concat_axis=0, tiled=True)
-    (near,) = call(
-        gather_kernel,
-        "gather",
-        [smem, anywhere, anywhere],
-        [(shape(z.near * width, 2 * width, dtype=BF16), vmem)],
-        [
-            pltpu.VMEM((z.near, width, width), F32),
-            pltpu.SemaphoreType.DMA((z.near,)),
-        ],
-        (ids, coupling, block_diag),
-        2 * tile_bytes + 4,
-    )
-    send, state, info, scalars = call(
+    send, state, info, scalars, near, mass = call(
         first_kernel,
         "first",
-        [vmem] * 7,
+        [vmem] * 4 + [hbm] * 5,
         [
             (shape(z.devices, z.send_rows, width), vmem),
             (shape(2, z.padded, width), vmem),
             (shape(z.devices, 128), vmem),
             (shape(8, 128), vmem),
-        ],
-        [pltpu.VMEM((z.padded, width), F32)] * 2,
-        (received, near, far, defect, mass, row_meta, col_meta),
-        2 * tile_bytes + 8,
+            (shape(z.near * width, 2 * width, dtype=BF16), vmem),
+            (shape(z.padded, width), vmem),
+        ],
+        [
+            pltpu.SMEM((2 * z.half + 2,), jnp.int32),
+            pltpu.VMEM((z.rows, width), F32),
+            pltpu.VMEM((z.rows, width), F32),
+            pltpu.VMEM((z.half, width, width), F32),
+            pltpu.VMEM((z.rows, width, width), F32),
+            pltpu.VMEM((z.padded, width), F32),
+            pltpu.VMEM((z.padded, width), F32),
+            pltpu.SemaphoreType.DMA((4,)),
+            pltpu.SemaphoreType.DMA((z.half,)),
+        ],
+        (received, far, row_meta, col_meta, ids, defect, mass, coupling, block_diag),
+        2 * z.near * tile // MIB + 4,
     )
     received = lax.all_to_all(send, "blk", split_axis=0, concat_axis=0, tiled=True)
     send, state, scalars = call(
@@ -569,9 +643,9 @@
             (shape(4, z.padded, width), vmem),
             (shape(8, 128), vmem),
         ],
-        [pltpu.VMEM((z.padded, width), F32)],
+        [],
         (received, near, far, mass, row_meta, col_meta, state, info, scalars),
-        2 * tile_bytes + 8,
+        4,
     )
     received = lax.all_to_all(send, "blk", split_axis=0, concat_axis=0, tiled=True)
     send, state, scalars = call(
@@ -583,9 +657,9 @@
             (shape(3, z.padded, width), vmem),
             (shape(8, 128), vmem),
         ],
-        [pltpu.VMEM((z.padded, width), F32)],
+        [],
         (received, near, mass, row_meta, col_meta, state, info, scalars),
-        2 * tile_bytes + 8,
+        4,
     )
     received = lax.all_to_all(send, "blk", split_axis=0, concat_axis=0, tiled=True)
     (update,) = call(

time: 84.9 us -> 64.3 us (0.76)
  blocking collectives: 32.8 us -> 47 us
  Pallas kernels: 31 us -> 17 us
  local copies, waits for them, and re-layouts: 13.4 us -> 0 us
  starting transfers between devices: 7.33 us -> 0 us
    all_to_all x3 -> x4, blocking collectives: 32.8 us -> 47 us  [on_device(): lax.all_to_all(send, 'blk', split_axis=0, concat_axis=0, tiled=True)]
    pallas_call x6 -> x5, Pallas kernels: 31 us -> 17 us  [call(): pl.pallas_call(functools.partial(kernel, z), out_shape=[item[0] for item...]
    unnamed x24 -> x0, local copies, waits for them, and re-layouts: 13.4 us -> none
    all_to_all x1 -> x0, starting transfers between devices: 7.33 us -> none  [on_device(): lax.all_to_all(send, 'blk', split_axis=0, concat_axis=0, tiled=True)]
  transfers between devices with their start and end apart: 1 -> 0, of which waited for: 0 -> 0; matrix products, arithmetic and copies ran while one was open for 0% -> 0% of each run, Pallas kernels for 8% -> 0%
where the time goes in v2:
time: 64.3 us; the launch traced here: 64 us
  blocking collectives  47 us (73%)
  Pallas kernels  17 us (26%)
    all_to_all x4, blocking collectives, on_device(): lax.all_to_all(send, 'blk', split_axis=0, concat_axis=0, tiled=True)  47 us
    pallas_call x5, Pallas kernels, call(): pl.pallas_call(functools.partial(kernel, z), out_shape=[item[0] for item...  17 us

profile of v2, /device:TPU:0, one launch (start us, length us, event | category | flops | bytes accessed | tf_op | source)
XLA Modules:
  0.0 64.0 jit_solution(13579982074864438709)
XLA Ops:
  0.0 5.1 %prepare.1 = (f32[32,16,128]{2,1,0:T(8,128)S(1)}, bf16[6144,256]{1,0:T(8,128)(2,1)S(1)}, f32[8,128]{1,0:T(8,128)S(1)}, f32[64,128]{1,0:T(8,128)S(1)}, s32[98]{0:T(128)S(1)}) custom-call(s32[96]{0:T(128)} %rows_hbm.1, s32[1,96]{1,0:T(1,128)} %bitcast.2, s32[1,96]{1,0:T(1,128)} %bitcast.3, f32[12,128]{1,0:T(8,128)} %defect_hbm.3, f32[96,128,128]{2,1,0:T(8,128)} %coupling_hbm.3), custom_call_target="tpu_custom_call" | custom-call | tf_op jit(solution)/shard_map/prepare/pallas_call | solution.py:564
  5.1 17.7 %all_to_all.20.received_ref = f32[32,16,128]{2,1,0:T(8,128)S(1)} all-to-all(f32[32,16,128]{2,1,0:T(8,128)S(1)} %get-tuple-element.22), channel_id=1, replica_groups=mesh['blk'=32] {'blk'}, dimensions={0} | all-to-all | bytes 524288 | tf_op jit(solution)/shard_map/all_to_all | solution.py:609
  22.8 6.0 %first.1 = (f32[32,5,128]{2,1,0:T(8,128)S(1)}, f32[2,16,128]{2,1,0:T(8,128)S(1)}, f32[32,128]{1,0:T(8,128)S(1)}, f32[8,128]{1,0:T(8,128)S(1)}, bf16[7680,256]{1,0:T(8,128)(2,1)S(1)}, /*index=5*/f32[16,128]{1,0:T(8,128)S(1)}) custom-call(f32[32,16,128]{2,1,0:T(8,128)S(1)} %all_to_all.20.received_ref, bf16[6144,256]{1,0:T(8,128)(2,1)S(1)} %get-tuple-element.23.far_ref, ...), custom_call_target="tpu_custom_call" | custom-call | tf_op jit(solution)/shard_map/first/pallas_call | solution.py:564
  28.9 10.4 %all_to_all.21.received_ref = f32[32,5,128]{2,1,0:T(8,128)S(1)} all-to-all(f32[32,5,128]{2,1,0:T(8,128)S(1)} %get-tuple-element.27), channel_id=1, replica_groups=mesh['blk'=32] {'blk'}, dimensions={0} | all-to-all | bytes 163840 | tf_op jit(solution)/shard_map/all_to_all | solution.py:636
  39.3 2.9 %second.1 = (f32[32,5,128]{2,1,0:T(8,128)S(1)}, f32[4,16,128]{2,1,0:T(8,128)S(1)}, f32[8,128]{1,0:T(8,128)S(1)}) custom-call(f32[32,5,128]{2,1,0:T(8,128)S(1)} %all_to_all.21.received_ref, bf16[7680,256]{1,0:T(8,128)(2,1)S(1)} %get-tuple-element.28.near_ref, bf16[6144,256]{1,0:T(8,128)(2,1)S(1)} %get-tuple-element.23.far_ref, ...), custom_call_target="tpu_custom_call" | custom-call | tf_op jit(solution)/shard_map/second/pallas_call | solution.py:564
  42.2 10.0 %all_to_all.22.received_ref = f32[32,5,128]{2,1,0:T(8,128)S(1)} all-to-all(f32[32,5,128]{2,1,0:T(8,128)S(1)} %get-tuple-element.33), channel_id=1, replica_groups=mesh['blk'=32] {'blk'}, dimensions={0} | all-to-all | bytes 163840 | tf_op jit(solution)/shard_map/all_to_all | solution.py:650
  52.1 1.6 %third.1 = (f32[32,1,128]{2,1,0:T(1,128)S(1)}, f32[3,16,128]{2,1,0:T(8,128)S(1)}, f32[8,128]{1,0:T(8,128)S(1)}) custom-call(f32[32,5,128]{2,1,0:T(8,128)S(1)} %all_to_all.22.received_ref, bf16[7680,256]{1,0:T(8,128)(2,1)S(1)} %get-tuple-element.28.near_ref, f32[16,128]{1,0:T(8,128)S(1)} %get-tuple-element.29.mass_ref, ...), custom_call_target="tpu_custom_call" | custom-call | tf_op jit(solution)/shard_map/third/pallas_call | solution.py:564
  53.8 8.9 %all_to_all.23.received_ref = f32[32,1,128]{2,1,0:T(1,128)S(1)} all-to-all(f32[32,1,128]{2,1,0:T(1,128)S(1)} %get-tuple-element.36), channel_id=1, replica_groups=mesh['blk'=32] {'blk'}, dimensions={0} | all-to-all | bytes 32768 | tf_op jit(solution)/shard_map/all_to_all | solution.py:664
  62.7 1.3 %last.1 = f32[12,128]{1,0:T(8,128)} custom-call(f32[32,1,128]{2,1,0:T(1,128)S(1)} %all_to_all.23.received_ref, f32[3,16,128]{2,1,0:T(8,128)S(1)} %get-tuple-element.37.state_in, f32[8,128]{1,0:T(8,128)S(1)} %get-tuple-element.38.scalar_in), custom_call_target="tpu_custom_call" | custom-call | tf_op jit(solution)/shard_map/last/pallas_call | solution.py:564

commit v3 on v0

v3 whole, which is shorter than its diff:
```python
import functools

import jax
import jax.numpy as jnp
from jax import lax
from jax.experimental import pallas as pl
from jax.experimental.pallas import tpu as pltpu
from jax.sharding import PartitionSpec as P

F32 = jnp.float32
BF16 = jnp.bfloat16
NT = (((1,), (1,)), ((), ()))
NN = (((1,), (0,)), ((), ()))
FLOOR = 2.0**-22
MIB = 1 << 20
CHUNK = 32
OCTET = 8


def round_up(value, step):
    return -(-value // step) * step


class Sizes:
    def __init__(self, devices, rows, width, tiles):
        self.devices = devices
        self.rows = rows
        self.width = width
        self.tiles = tiles
        self.half = tiles // 2
        self.near = self.half + rows
        self.slots = (self.half + devices - 2) // (devices - 1)
        self.cells = self.slots * devices
        self.padded = round_up(rows, 16)
        self.near_rows = 2 * round_up(self.near, OCTET)
        self.far_rows = 2 * round_up(self.half, OCTET)
        self.first_rows = rows + self.slots + 1
        self.info_row = rows + self.slots
        self.send_rows = 2 * self.slots + 1
        self.dots_row = 2 * self.slots


def dot(a, b, dims=NN):
    return lax.dot_general(a, b, dims, preferred_element_type=F32)


def split(value):
    high = value.astype(BF16)
    low = (value - high.astype(F32)).astype(BF16)
    return high, low


def both(value):
    return jnp.concatenate(split(value), axis=1)


def exact_dot(onehot, value):
    width = value.shape[1]
    out = dot(onehot, both(value))
    return out[:, :width] + out[:, width:]


def iota(shape, axis):
    return lax.broadcasted_iota(jnp.int32, shape, axis)


def fiota(shape, axis):
    return iota(shape, axis).astype(F32)


def total(value):
    return jnp.sum(jnp.sum(value, axis=0, keepdims=True), axis=1, keepdims=True)


def lane_row(values):
    lane = iota((1, 128), 1)
    row = jnp.zeros((1, 128), F32)
    for index, value in enumerate(values):
        row = jnp.where(lane == index, value, row)
    return row


def lane_values(row, count):
    return [jnp.broadcast_to(row[:, i : i + 1], (1, 128)) for i in range(count)]


def store_tile(tiles_ref, index, tile):
    width = tile.shape[0]
    high, low = split(tile.T)
    base = 2 * width * index
    tiles_ref[base : base + width, :] = high
    tiles_ref[base + width : base + 2 * width, :] = low


def tile_inputs(source_index, source):
    rows = source_index.shape[0]
    width = source.shape[1]
    onehot = (fiota((rows, source.shape[0]), 1) == source_index).astype(BF16)
    out = dot(onehot, both(source))
    odd = (iota((rows, width), 0) & 1) == 1
    picked = jnp.where(odd, out[:, width:], out[:, :width]).astype(BF16)
    return jnp.concatenate([picked, picked], axis=1)


def octet_products(tiles_ref, inputs, octet, count):
    width = inputs.shape[1] // 2
    left = inputs[2 * OCTET * octet : 2 * OCTET * (octet + 1), :]
    sub = iota((2 * OCTET, width), 0)
    acc = jnp.zeros((2 * OCTET, width), F32)
    for j in range(OCTET // 2):
        tile = OCTET * octet + 2 * j
        if tile >= count:
            break
        pair = [
            tiles_ref[2 * width * t : 2 * width * (t + 1), :]
            for t in range(tile, min(tile + 2, count))
        ]
        out = dot(left, jnp.concatenate(pair, axis=1))
        for i in range(len(pair)):
            mine = (sub >> 1) == 2 * j + i
            acc = jnp.where(mine, out[:, i * width : (i + 1) * width], acc)
    return acc


def tile_products(tiles_ref, inputs, count):
    octets = inputs.shape[0] // (2 * OCTET)
    return jnp.concatenate(
        [octet_products(tiles_ref, inputs, o, count) for o in range(octets)], axis=0
    )


def sum_products(targets, count, products):
    select = (fiota((count, products.shape[0]), 0) == targets).astype(BF16)
    return exact_dot(select, products)


def every(ref, start, count, step):
    return ref[pl.ds(start, count, stride=step), :]


def prepare_kernel(
    z,
    rows_hbm,
    rows_2d_hbm,
    cols_2d_hbm,
    defect_hbm,
    mass_hbm,
    coupling_hbm,
    diag_hbm,
    send_ref,
    far_ref,
    row_meta_ref,
    near_meta_ref,
    far_meta_ref,
    own_ref,
    ids_out,
    tiles_ref,
    diag_ref,
    ids_ref,
    rows_smem,
    rows_ref,
    cols_ref,
    defect_ref,
    mass_ref,
    index,
    small_sems,
    sems,
):
    me = lax.axis_index("blk")
    base = me * z.rows
    width = z.width
    small = [
        pltpu.make_async_copy(source, target, small_sems.at[i])
        for i, (source, target) in enumerate(
            [
                (rows_hbm, rows_smem),
                (rows_2d_hbm, rows_ref),
                (cols_2d_hbm, cols_ref),
                (defect_hbm, defect_ref),
            ]
        )
    ]
    for copy in small:
        copy.start()
    zero = (me * 7 + 3) // (7 * z.devices + 5)
    chunks = []
    for i, start in enumerate(range(0, z.tiles, CHUNK)):
        part = pl.ds(start + zero, min(CHUNK, z.tiles - start))
        chunks.append(
            pltpu.make_async_copy(
                coupling_hbm.at[part], tiles_ref.at[part], sems.at[i]
            )
        )
    diag_copy = pltpu.make_async_copy(diag_hbm, diag_ref, sems.at[len(chunks)])
    mass_copy = pltpu.make_async_copy(mass_hbm, mass_ref, small_sems.at[4])
    for copy in chunks + [diag_copy, mass_copy]:
        copy.start()
    own_ref[...] = jnp.zeros_like(own_ref)
    index[...] = jnp.full(index.shape, -1, jnp.int32)
    small[0].wait()

    near = jnp.int32(0)
    far = jnp.int32(0)
    for t in range(z.tiles):
        row = rows_smem[t]
        here = ((row >= base) & (row < base + z.rows)).astype(jnp.int32)
        ids_ref[near] = jnp.int32(t)
        ids_ref[z.half + 1 + far] = jnp.int32(t)
        near = near + here
        far = far + 1 - here

    ids_copy = pltpu.make_async_copy(ids_ref, ids_out, small_sems.at[5])
    ids_copy.start()
    for copy in small[1:]:
        copy.wait()
    own_ref[0, 0 : z.rows, :] = defect_ref[...]
    defect = own_ref[0]

    count = index.shape[1]
    index[0:1, 0 : z.tiles] = rows_ref[...]
    index[1:2, 0 : z.tiles] = cols_ref[...]
    rows = index[0:1, :].astype(F32)
    cols = index[1:2, :].astype(F32)
    valid = rows >= 0
    row_owner = jnp.floor((rows + 0.5) * (1.0 / z.rows))
    col_owner = jnp.floor((cols + 0.5) * (1.0 / z.rows))
    row_local = rows - row_owner * z.rows
    col_local = cols - col_owner * z.rows
    mine = me.astype(F32)
    is_far = valid & (row_owner != mine)
    is_near = valid & (row_owner == mine)
    far_owner = jnp.where(is_far, row_owner, col_owner)
    far_local = jnp.where(is_far, row_local, col_local)
    own_local = jnp.where(is_far, col_local, row_local)
    kind = jnp.where(is_far, 1.0, jnp.where(is_near, 0.0, -1.0))
    key = jnp.where(valid, kind * z.devices + far_owner, -1.0)
    square = (count, count)
    before = iota(square, 0) < iota(square, 1)

    def ranks(value):
        wide = jnp.broadcast_to(value, square)
        same = (wide.T == wide) & before
        return jnp.sum(same.astype(F32), axis=0, keepdims=True)

    slot = ranks(key)
    position = ranks(kind)
    facts = jnp.concatenate(
        [
            far_owner,
            far_local,
            own_local,
            slot,
            jnp.ones((1, count), F32),
            jnp.zeros((3, count), F32),
        ],
        axis=0,
    )
    facts = jnp.where(valid, facts, 0.0).astype(BF16)

    def listed(members, rows_in_list):
        tile = (iota((rows_in_list, count), 0) >> 1).astype(F32)
        pick = ((position == tile) & members).astype(BF16)
        return dot(facts, pick, NT), dot(pick, facts, NT)

    near_row, near_col = listed(is_near, z.near_rows)
    far_row, far_col = listed(is_far, z.far_rows)

    place_row = (iota((1, z.near_rows), 1) >> 1).astype(F32) - z.half
    diag_row = (place_row >= 0) & (place_row < z.rows)
    near_target = jnp.where(near_row[4:5, :] > 0, near_row[2:3, :], -1.0)
    near_target = jnp.where(diag_row, place_row, near_target)
    far_target = far_row[3:4, :] * z.devices + far_row[0:1, :]
    far_target = jnp.where(far_row[4:5, :] > 0, far_target, -1.0)
    row_meta_ref[...] = jnp.full(row_meta_ref.shape, -1.0, F32)
    row_meta_ref[0:1, 0 : z.near_rows] = near_target
    row_meta_ref[1:2, 0 : z.far_rows] = far_target

    place_col = (iota((z.near_rows, 1), 0) >> 1).astype(F32) - z.half
    diag_col = (place_col >= 0) & (place_col < z.rows)
    real = near_col[:, 4:5] > 0
    first_source = near_col[:, 0:1] * z.first_rows + near_col[:, 1:2]
    first_source = jnp.where(real, first_source, -1.0)
    first_source = jnp.where(diag_col, mine * z.first_rows + place_col, first_source)
    later_source = near_col[:, 0:1] * z.send_rows + near_col[:, 3:4]
    later_source = jnp.where(real, later_source, -1.0)
    later_source = jnp.where(
        diag_col, z.devices * z.send_rows + place_col, later_source
    )
    lane = iota((z.near_rows, 128), 1)
    near_meta_ref[...] = jnp.where(lane == 0, first_source, later_source)
    far_source = jnp.where(far_col[:, 4:5] > 0, far_col[:, 2:3], -1.0)
    far_meta_ref[...] = jnp.broadcast_to(far_source, (z.far_rows, 128))

    def told(row_facts, col_facts, offset):
        shape = (col_facts.shape[0], 128)
        once = (iota(shape, 0) & 1) == 0
        match = (fiota(shape, 1) == col_facts[:, 3:4] + offset) & once
        told_value = jnp.where(match & (col_facts[:, 4:5] > 0), col_facts[:, 1:2] + 1.0, 0.0)
        owner = fiota((z.devices, row_facts.shape[1]), 0)
        return dot((owner == row_facts[0:1, :]).astype(BF16), told_value.astype(BF16))

    info = told(near_row, near_col, 0) + told(far_row, far_col, z.slots)
    for r in range(z.rows):
        send_ref[pl.ds(r, z.devices, stride=z.first_rows), :] = jnp.broadcast_to(
            defect[r : r + 1, :], (z.devices, width)
        )
    send_ref[pl.ds(z.info_row, z.devices, stride=z.first_rows), :] = info

    inputs = tile_inputs(far_source, defect)
    arrived = 0
    parts = []
    for octet in range(z.far_rows // (2 * OCTET)):
        group = range(OCTET * octet, min(OCTET * (octet + 1), z.half))
        needed = min(-(-(z.half + group[-1] + 1) // CHUNK), len(chunks))
        while arrived < needed:
            chunks[arrived].wait()
            arrived += 1
        for k in group:
            store_tile(far_ref, k, tiles_ref[ids_ref[z.half + 1 + k]])
        parts.append(octet_products(far_ref, inputs, octet, z.half))
    while arrived < len(chunks):
        chunks[arrived].wait()
        arrived += 1
    pushes = sum_products(far_target, z.cells, jnp.concatenate(parts, axis=0))
    for s in range(z.slots):
        send_ref[pl.ds(z.rows + s, z.devices, stride=z.first_rows), :] = pushes[
            s * z.devices : (s + 1) * z.devices
        ]
    ids_copy.wait()
    mass_copy.wait()
    own_ref[1, 0 : z.rows, :] = mass_ref[...]
    diag_copy.wait()


def fill_send(z, send_ref, ask_ref, far_ref, far_source, far_target, vector, dots):
    asked = exact_dot(ask_ref[...], vector)
    for s in range(z.slots):
        send_ref[pl.ds(s, z.devices, stride=z.send_rows), :] = asked[
            s * z.devices : (s + 1) * z.devices
        ]
    send_ref[pl.ds(z.dots_row, z.devices, stride=z.send_rows), :] = jnp.broadcast_to(
        lane_row(dots), (z.devices, 128)
    )
    inputs = tile_inputs(far_source, vector)
    products = tile_products(far_ref, inputs, z.half)
    pushes = sum_products(far_target, z.cells, products)
    for s in range(z.slots):
        send_ref[pl.ds(z.slots + s, z.devices, stride=z.send_rows), :] = pushes[
            s * z.devices : (s + 1) * z.devices
        ]


def landed(z, received_ref, land, start, step):
    received = [every(received_ref, start + s, z.devices, step) for s in range(z.slots)]
    return exact_dot(land, jnp.concatenate(received, axis=0))


def first_kernel(
    z,
    received_ref,
    tiles_ref,
    diag_ref,
    far_ref,
    own_ref,
    row_meta_ref,
    near_meta_ref,
    far_meta_ref,
    ids_in,
    send_ref,
    near_ref,
    state_ref,
    ask_ref,
    land_ref,
    scalar_ref,
    ids_ref,
    ids_sem,
):
    width = z.width
    ids_copy = pltpu.make_async_copy(ids_in, ids_ref, ids_sem)
    ids_copy.start()
    defect = own_ref[0]
    mass = own_ref[1]
    squares = jnp.zeros((z.devices, width), F32)
    for r in range(z.rows):
        block = every(received_ref, r, z.devices, z.first_rows)
        squares = squares + block * block
    beta_square = total(squares)
    scale = -lax.rsqrt(beta_square)
    scalar_ref[...] = jnp.broadcast_to(jnp.sqrt(beta_square), scalar_ref.shape)

    info = every(received_ref, z.info_row, z.devices, z.first_rows)
    ask, land = [], []
    for s in range(z.slots):
        lanes = fiota((z.devices, 128), 1)
        ask.append((lanes == info[:, s : s + 1] - 1.0).astype(F32))
        land.append(
            (lanes == info[:, z.slots + s : z.slots + s + 1] - 1.0).astype(F32)
        )
    ask_ref[...] = jnp.concatenate(ask, axis=0)[:, : z.padded].astype(BF16)
    land_mark = jnp.concatenate(land, axis=0).T[: z.padded, :].astype(BF16)
    land_ref[...] = land_mark

    inputs = tile_inputs(near_meta_ref[:, 0:1], received_ref[...])
    octets = z.near_rows // (2 * OCTET)
    parts = [None] * octets
    waited = False
    for octet in sorted(range(octets), key=lambda o: o < z.half // OCTET):
        for k in range(OCTET * octet, min(OCTET * (octet + 1), z.near)):
            if k < z.half and not waited:
                ids_copy.wait()
                waited = True
            tile = tiles_ref[ids_ref[k]] if k < z.half else diag_ref[k - z.half]
            store_tile(near_ref, k, tile)
        parts[octet] = octet_products(near_ref, inputs, octet, z.near)
    products = jnp.concatenate(parts, axis=0)
    image = mass * defect
    image = image + landed(z, received_ref, land_mark, z.rows, z.first_rows)
    image = image + sum_products(
        row_meta_ref[0:1, : z.near_rows], z.padded, products
    )
    v0 = defect * scale
    w0 = image * scale
    dots = [total(w0 * v0), total(w0 * w0)]
    state_ref[0] = v0
    state_ref[1] = w0
    fill_send(
        z,
        send_ref,
        ask_ref,
        far_ref,
        far_meta_ref[:, 0:1],
        row_meta_ref[1:2, : z.far_rows],
        w0,
        dots,
    )


def apply_received(
    z, received_ref, near_ref, own_ref, row_meta_ref, near_meta_ref, land_ref, vector
):
    source = jnp.concatenate([received_ref[...], vector], axis=0)
    inputs = tile_inputs(near_meta_ref[:, 1:2], source)
    products = tile_products(near_ref, inputs, z.near)
    image = own_ref[1] * vector
    image = image + landed(z, received_ref, land_ref[...], z.slots, z.send_rows)
    return image + sum_products(row_meta_ref[0:1, : z.near_rows], z.padded, products)


def second_kernel(
    z,
    received_ref,
    near_ref,
    far_ref,
    own_ref,
    row_meta_ref,
    near_meta_ref,
    far_meta_ref,
    ask_ref,
    land_ref,
    state_in,
    scalar_in,
    send_ref,
    state_ref,
    scalar_ref,
):
    v0 = state_in[0]
    w0 = state_in[1]
    received_dots = every(received_ref, z.dots_row, z.devices, z.send_rows)
    sums = jnp.sum(received_dots, axis=0, keepdims=True)
    h00, g00 = lane_values(sums, 2)
    inverse = lax.rsqrt(jnp.maximum(g00 - h00 * h00, FLOOR * g00))
    v1 = (w0 - h00 * v0) * inverse
    image = apply_received(
        z, received_ref, near_ref, own_ref, row_meta_ref, near_meta_ref, land_ref, w0
    )
    w1 = (image - h00 * w0) * inverse
    dots = [total(w1 * v0), total(w1 * v1), total(w1 * w1), total(w1 * w0)]
    state_ref[0] = v0
    state_ref[1] = v1
    state_ref[2] = w0
    state_ref[3] = w1
    scalar_ref[...] = jnp.broadcast_to(
        lane_row([scalar_in[0:1, 0:1], h00, g00]), scalar_ref.shape
    )
    fill_send(
        z,
        send_ref,
        ask_ref,
        far_ref,
        far_meta_ref[:, 0:1],
        row_meta_ref[1:2, : z.far_rows],
        w1,
        dots,
    )


def third_kernel(
    z,
    received_ref,
    near_ref,
    own_ref,
    row_meta_ref,
    near_meta_ref,
    land_ref,
    state_in,
    scalar_in,
    send_ref,
    state_ref,
    scalar_ref,
):
    v0, v1, w0, w1 = state_in[0], state_in[1], state_in[2], state_in[3]
    received_dots = every(received_ref, z.dots_row, z.devices, z.send_rows)
    sums = jnp.sum(received_dots, axis=0, keepdims=True)
    h01, h11, g11, g01 = lane_values(sums, 4)
    inverse = lax.rsqrt(jnp.maximum(g11 - h01 * h01 - h11 * h11, FLOOR * g11))
    v2 = (w1 - h01 * v0 - h11 * v1) * inverse
    beta, h00, g00 = lane_values(scalar_in[0:1, :], 3)
    i00 = lax.rsqrt(g00)
    l10 = g01 * i00
    i11 = lax.rsqrt(g11 - l10 * l10)
    f0 = beta * h00 * i00
    f1 = (beta * h01 - l10 * f0) * i11
    image = apply_received(
        z, received_ref, near_ref, own_ref, row_meta_ref, near_meta_ref, land_ref, w1
    )
    w2 = (image - h01 * w0 - h11 * w1) * inverse
    dots = [total(w2 * v0), total(w2 * w0), total(w2 * w1), total(w2 * w2)]
    state_ref[0] = v0
    state_ref[1] = v1
    state_ref[2] = v2
    for row, value in enumerate([beta, i00, l10, i11, f0, f1]):
        scalar_ref[row : row + 1, :] = value
    send_ref[...] = jnp.broadcast_to(lane_row(dots), (z.devices, 128))


def last_kernel(z, received_ref, state_in, scalar_in, out_ref):
    sums = jnp.sum(received_ref[...], axis=0, keepdims=True)
    d, g02, g12, g22 = lane_values(sums, 4)
    beta, i00, l10, i11, f0, f1 = [scalar_in[row : row + 1, :] for row in range(6)]
    l20 = g02 * i00
    l21 = (g12 - l20 * l10) * i11
    y2 = (beta * d - l20 * f0 - l21 * f1) / (g22 - l20 * l20 - l21 * l21)
    y1 = (f1 - l21 * y2) * i11
    y0 = (f0 - l10 * y1 - l20 * y2) * i00
    update = y0 * state_in[0] + y1 * state_in[1] + y2 * state_in[2]
    out_ref[...] = update[0 : z.rows, :]


def exchange(z, value):
    rows, width = value.shape
    value = value.reshape(z.devices, 1, rows // z.devices * width)
    value = lax.all_to_all(value, "blk", split_axis=0, concat_axis=0, tiled=True)
    return value.reshape(rows, width)


def on_device(defect, mass, block_diag, coupling, tile_rows, tile_cols):
    z = Sizes(lax.axis_size("blk"), defect.shape[0], defect.shape[1], tile_rows.shape[0])
    width = z.width
    vmem = pl.BlockSpec(memory_space=pltpu.VMEM)
    hbm = pl.BlockSpec(memory_space=pltpu.HBM)

    def shape(*dims, dtype=F32):
        return jax.ShapeDtypeStruct(dims, dtype)

    def in_hbm(value):
        return pltpu.with_memory_space_constraint(value, pltpu.HBM)

    def call(kernel, name, ins, outs, scratch, args, limit=4):
        return pl.pallas_call(
            functools.partial(kernel, z),
            out_shape=outs,
            in_specs=ins,
            out_specs=[vmem] * len(outs),
            scratch_shapes=scratch,
            name=name,
            compiler_params=pltpu.CompilerParams(vmem_limit_bytes=limit * MIB),
        )(*args)

    def pieces(count):
        return shape(2 * count * width, width, dtype=BF16)

    rows_2d = tile_rows.reshape(1, z.tiles)
    cols_2d = tile_cols.reshape(1, z.tiles)
    send, far, row_meta, near_meta, far_meta, own, ids, tiles, diag = call(
        prepare_kernel,
        "prepare",
        [hbm] * 7,
        [
            shape(z.devices * z.first_rows, width),
            pieces(z.half),
            shape(8, round_up(max(z.near_rows, z.far_rows), 128)),
            shape(z.near_rows, 128),
            shape(z.far_rows, 128),
            shape(2, z.padded, width),
            shape(2 * z.half + 2, dtype=jnp.int32),
            shape(z.tiles, width, width),
            shape(z.rows, width, width),
        ],
        [
            pltpu.SMEM((2 * z.half + 2,), jnp.int32),
            pltpu.SMEM((z.tiles,), jnp.int32),
            pltpu.VMEM((1, z.tiles), jnp.int32),
            pltpu.VMEM((1, z.tiles), jnp.int32),
            pltpu.VMEM((z.rows, width), F32),
            pltpu.VMEM((z.rows, width), F32),
            pltpu.VMEM((8, round_up(z.tiles, 128)), jnp.int32),
            pltpu.SemaphoreType.DMA((6,)),
            pltpu.SemaphoreType.DMA((-(-z.tiles // CHUNK) + 1,)),
        ],
        map(in_hbm, (tile_rows, rows_2d, cols_2d, defect, mass, coupling, block_diag)),
    )
    received = exchange(z, send)
    send, near, state, ask, land, scalars = call(
        first_kernel,
        "first",
        [vmem] * 9,
        [
            shape(z.devices * z.send_rows, width),
            pieces(z.near),
            shape(2, z.padded, width),
            shape(z.cells, z.padded, dtype=BF16),
            shape(z.padded, z.cells, dtype=BF16),
            shape(8, 128),
        ],
        [pltpu.SMEM((2 * z.half + 2,), jnp.int32), pltpu.SemaphoreType.DMA],
        (received, tiles, diag, far, own, row_meta, near_meta, far_meta, ids),
    )
    received = exchange(z, send)
    send, state, scalars = call(
        second_kernel,
        "second",
        [vmem] * 11,
        [
            shape(z.devices * z.send_rows, width),
            shape(4, z.padded, width),
            shape(8, 128),
        ],
        [],
        (
            received,
            near,
            far,
            own,
            row_meta,
            near_meta,
            far_meta,
            ask,
            land,
            state,
            scalars,
        ),
    )
    received = exchange(z, send)
    send, state, scalars = call(
        third_kernel,
        "third",
        [vmem] * 8,
        [
            shape(z.devices, width),
            shape(3, z.padded, width),
            shape(8, 128),
        ],
        [],
        (received, near, own, row_meta, near_meta, land, state, scalars),
    )
    received = exchange(z, send)
    (update,) = call(
        last_kernel,
        "last",
        [vmem] * 3,
        [shape(z.rows, width)],
        [],
        (received, state, scalars),
    )
    return update


def solution(mesh):
    in_specs = (
        P("blk", None),
        P("blk", None),
        P("blk", None, None),
        P("blk", None, None),
        P("blk"),
        P("blk"),
    )
    return jax.shard_map(
        on_device, mesh=mesh, in_specs=in_specs, out_specs=P("blk", None), check_vma=False
    )
```

time: 496 us -> 55.8 us (0.11)
  blocking collectives: 277 us -> 45.3 us
  local copies, waits for them, and re-layouts: 64.7 us -> 0 us
  matrix products: 42.4 us -> 0 us
  waiting for transfers between devices: 40.1 us -> 0 us
  starting transfers between devices: 32.3 us -> 0 us
  other arithmetic: 25.1 us -> 0 us
  between operations: 12.6 us -> 0.03 us
  Pallas kernels: 0 us -> 10.2 us
    psum x7 -> x0, blocking collectives: 277 us -> none  [the longest x3 121 us: on_device(): norm = jnp.sqrt(lax.psum(jnp.sum(image * image), 'blk'))]
    scatter x11 -> x0, local copies, waits for them, and re-layouts: 47.7 us -> none  [the longest x3 34 us: on_device(): outgoing = jnp.zeros((devices, slots, width), jnp.float32).at[push_lane,...]
    all_to_all x0 -> x4, blocking collectives: none -> 45.3 us  [exchange(): lax.all_to_all(value, 'blk', split_axis=0, concat_axis=0, tiled=True)]
    dot_general x13 -> x0, matrix products: 42.4 us -> none  [the longest x3 35.5 us: tile_products(): jnp.einsum('tij,tj->ti', coupling, inputs, precision=lax.Precision.HIGHEST)]
    all_to_all x8 -> x0, waiting for transfers between devices: 40.1 us -> none  [the longest x3 21.4 us: on_device(): lax.all_to_all(outgoing, 'blk', split_axis=0, concat_axis=0, tiled=True)]
    all_to_all x8 -> x0, starting transfers between devices: 32.3 us -> none  [the longest x3 12.6 us: on_device(): lax.all_to_all(apply_vector[asked], 'blk', split_axis=0, concat_axis=0, t...]
    another operation x12 -> x0, other arithmetic: 10.4 us -> none
    pallas_call x0 -> x5, Pallas kernels: none -> 10.2 us  [call(): pl.pallas_call(functools.partial(kernel, z), out_shape=outs, in_specs=ins...]
  transfers between devices with their start and end apart: 8 -> 0, of which waited for: 7 -> 0; matrix products, arithmetic and copies ran while one was open for 4% -> 0% of each run, Pallas kernels for 0% -> 0%
where the time goes in v3:
time: 55.8 us; the launch traced here: 55.6 us
  blocking collectives  45.3 us (81%)
  Pallas kernels  10.2 us (18%)
    all_to_all x4, blocking collectives, exchange(): lax.all_to_all(value, 'blk', split_axis=0, concat_axis=0, tiled=True)  45.3 us
    pallas_call x5, Pallas kernels, call(): pl.pallas_call(functools.partial(kernel, z), out_shape=outs, in_specs=ins...  10.2 us

profile of v3, /device:TPU:0, one launch (start us, length us, event | category | flops | bytes accessed | tf_op | source)
XLA Modules:
  0.0 55.6 jit_solution(6039995556217486467)
XLA Ops:
  0.0 4.1 %prepare.1 = (f32[480,128]{1,0:T(8,128)S(1)}, bf16[12288,128]{1,0:T(8,128)(2,1)S(1)}, f32[8,128]{1,0:T(8,128)S(1)}, f32[128,128]{1,0:T(8,128)S(1)}, f32[96,128]{...) custom-call(s32[96]{0:T(128)} %rows_hbm.1, ...), custom_call_target="tpu_custom_call" | custom-call | tf_op jit(solution)/shard_map/prepare/pallas_call | solution.py:569
  4.1 17.4 %all_to_all.20 = f32[32,1,1920]{2,1,0:T(1,128)S(1)} all-to-all(f32[32,1,1920]{2,1,0:T(1,128)S(1)} %bitcast.15), channel_id=1, replica_groups=mesh['blk'=32] {'blk'}, dimensions={0} | all-to-all | bytes 491520 | tf_op jit(solution)/shard_map/all_to_all | solution.py:552
  21.5 2.8 %first.1 = (f32[160,128]{1,0:T(8,128)S(1)}, bf16[15360,128]{1,0:T(8,128)(2,1)S(1)}, f32[2,16,128]{2,1,0:T(8,128)S(1)}, bf16[64,16]{1,0:T(8,128)(2,1)S(1)}, bf16[...) custom-call(f32[480,128]{1,0:T(8,128)S(1)} %bitcast.12, f32[96,128,128]{2,1,0:T(8,128)S(1)} %get-tuple-element.27.tiles_ref, ...), custom_call_target="tpu_custom_call" | custom-call | tf_op jit(solution)/shard_map/first/pallas_call | solution.py:569
  24.3 9.7 %all_to_all.21 = f32[32,1,640]{2,1,0:T(1,128)S(1)} all-to-all(f32[32,1,640]{2,1,0:T(1,128)S(1)} %bitcast.16), channel_id=1, replica_groups=mesh['blk'=32] {'blk'}, dimensions={0} | all-to-all | bytes 163840 | tf_op jit(solution)/shard_map/all_to_all | solution.py:552
  34.0 1.7 %second.1 = (f32[160,128]{1,0:T(8,128)S(1)}, f32[4,16,128]{2,1,0:T(8,128)S(1)}, f32[8,128]{1,0:T(8,128)S(1)}) custom-call(f32[160,128]{1,0:T(8,128)S(1)} %bitcast.13, bf16[15360,128]{1,0:T(8,128)(2,1)S(1)} %get-tuple-element.36.near_ref, bf16[12288,128]{1,0:T(8,128)(2,1)S(1)} %get-tuple-element.29.far_ref, f32[2,16,128]{2,1,0:T(8,128)S(1)} %get-tuple-element.30.own_ref, ...), custom_call_target="tpu_custom_call" | custom-call | tf_op jit(solution)/shard_map/second/pallas_call | solution.py:569
  35.7 9.3 %all_to_all.22 = f32[32,1,640]{2,1,0:T(1,128)S(1)} all-to-all(f32[32,1,640]{2,1,0:T(1,128)S(1)} %bitcast.17), channel_id=1, replica_groups=mesh['blk'=32] {'blk'}, dimensions={0} | all-to-all | bytes 163840 | tf_op jit(solution)/shard_map/all_to_all | solution.py:552
  45.0 1.0 %third.1 = (f32[32,128]{1,0:T(8,128)S(1)}, f32[3,16,128]{2,1,0:T(8,128)S(1)}, f32[8,128]{1,0:T(8,128)S(1)}) custom-call(f32[160,128]{1,0:T(8,128)S(1)} %bitcast.14, bf16[15360,128]{1,0:T(8,128)(2,1)S(1)} %get-tuple-element.36.near_ref, f32[2,16,128]{2,1,0:T(8,128)S(1)} %get-tuple-element.30.own_ref, f32[8,128]{1,0:T(8,128)S(1)} %get-tuple-element.31.row_meta_ref, ...), custom_call_target="tpu_custom_call" | custom-call | tf_op jit(solution)/shard_map/third/pallas_call | solution.py:569
  46.0 8.9 %all_to_all.23 = f32[32,1,128]{2,1,0:T(1,128)S(1)} all-to-all(f32[32,1,128]{2,1,0:T(1,128)S(1)} %bitcast.19), channel_id=1, replica_groups=mesh['blk'=32] {'blk'}, dimensions={0} | all-to-all | bytes 32768 | tf_op jit(solution)/shard_map/all_to_all | solution.py:552
  54.8 0.7 %last.1 = f32[12,128]{1,0:T(8,128)} custom-call(f32[32,128]{1,0:T(8,128)S(1)} %bitcast.18, f32[3,16,128]{2,1,0:T(8,128)S(1)} %get-tuple-element.45.state_in, f32[8,128]{1,0:T(8,128)S(1)} %get-tuple-element.46.scalar_in), custom_call_target="tpu_custom_call" | custom-call | tf_op jit(solution)/shard_map/last/pallas_call | solution.py:569

commit v4 on v3

--- a/solution.py
+++ b/solution.py
@@ -153,9 +153,8 @@
     near_meta_ref,
     far_meta_ref,
     own_ref,
-    ids_out,
+    near_list_ref,
     tiles_ref,
-    diag_ref,
     ids_ref,
     rows_smem,
     rows_ref,
@@ -191,7 +190,9 @@
                 coupling_hbm.at[part], tiles_ref.at[part], sems.at[i]
             )
         )
-    diag_copy = pltpu.make_async_copy(diag_hbm, diag_ref, sems.at[len(chunks)])
+    diag_copy = pltpu.make_async_copy(
+        diag_hbm, near_list_ref.at[pl.ds(z.half, z.rows)], sems.at[len(chunks)]
+    )
     mass_copy = pltpu.make_async_copy(mass_hbm, mass_ref, small_sems.at[4])
     for copy in chunks + [diag_copy, mass_copy]:
         copy.start()
@@ -200,17 +201,11 @@
     small[0].wait()
 
     near = jnp.int32(0)
-    far = jnp.int32(0)
     for t in range(z.tiles):
-        row = rows_smem[t]
-        here = ((row >= base) & (row < base + z.rows)).astype(jnp.int32)
-        ids_ref[near] = jnp.int32(t)
-        ids_ref[z.half + 1 + far] = jnp.int32(t)
-        near = near + here
-        far = far + 1 - here
-
-    ids_copy = pltpu.make_async_copy(ids_ref, ids_out, small_sems.at[5])
-    ids_copy.start()
+        offset = rows_smem[t] - base
+        here = (offset >= 0) & (offset < z.rows)
+        ids_ref[jnp.where(here, near, z.half + t - near)] = jnp.int32(t)
+        near = near + here.astype(jnp.int32)
     for copy in small[1:]:
         copy.wait()
     own_ref[0, 0 : z.rows, :] = defect_ref[...]
@@ -262,50 +257,54 @@
         pick = ((position == tile) & members).astype(BF16)
         return dot(facts, pick, NT), dot(pick, facts, NT)
 
-    near_row, near_col = listed(is_near, z.near_rows)
     far_row, far_col = listed(is_far, z.far_rows)
-
-    place_row = (iota((1, z.near_rows), 1) >> 1).astype(F32) - z.half
-    diag_row = (place_row >= 0) & (place_row < z.rows)
-    near_target = jnp.where(near_row[4:5, :] > 0, near_row[2:3, :], -1.0)
-    near_target = jnp.where(diag_row, place_row, near_target)
+    far_source = jnp.where(far_col[:, 4:5] > 0, far_col[:, 2:3], -1.0)
     far_target = far_row[3:4, :] * z.devices + far_row[0:1, :]
     far_target = jnp.where(far_row[4:5, :] > 0, far_target, -1.0)
-    row_meta_ref[...] = jnp.full(row_meta_ref.shape, -1.0, F32)
-    row_meta_ref[0:1, 0 : z.near_rows] = near_target
-    row_meta_ref[1:2, 0 : z.far_rows] = far_target
-
-    place_col = (iota((z.near_rows, 1), 0) >> 1).astype(F32) - z.half
-    diag_col = (place_col >= 0) & (place_col < z.rows)
-    real = near_col[:, 4:5] > 0
-    first_source = near_col[:, 0:1] * z.first_rows + near_col[:, 1:2]
-    first_source = jnp.where(real, first_source, -1.0)
-    first_source = jnp.where(diag_col, mine * z.first_rows + place_col, first_source)
-    later_source = near_col[:, 0:1] * z.send_rows + near_col[:, 3:4]
-    later_source = jnp.where(real, later_source, -1.0)
-    later_source = jnp.where(
-        diag_col, z.devices * z.send_rows + place_col, later_source
-    )
-    lane = iota((z.near_rows, 128), 1)
-    near_meta_ref[...] = jnp.where(lane == 0, first_source, later_source)
-    far_source = jnp.where(far_col[:, 4:5] > 0, far_col[:, 2:3], -1.0)
     far_meta_ref[...] = jnp.broadcast_to(far_source, (z.far_rows, 128))
 
-    def told(row_facts, col_facts, offset):
-        shape = (col_facts.shape[0], 128)
-        once = (iota(shape, 0) & 1) == 0
-        match = (fiota(shape, 1) == col_facts[:, 3:4] + offset) & once
-        told_value = jnp.where(match & (col_facts[:, 4:5] > 0), col_facts[:, 1:2] + 1.0, 0.0)
-        owner = fiota((z.devices, row_facts.shape[1]), 0)
-        return dot((owner == row_facts[0:1, :]).astype(BF16), told_value.astype(BF16))
-
-    info = told(near_row, near_col, 0) + told(far_row, far_col, z.slots)
-    for r in range(z.rows):
-        send_ref[pl.ds(r, z.devices, stride=z.first_rows), :] = jnp.broadcast_to(
-            defect[r : r + 1, :], (z.devices, width)
+    def describe():
+        near_row, near_col = listed(is_near, z.near_rows)
+
+        place_row = (iota((1, z.near_rows), 1) >> 1).astype(F32) - z.half
+        diag_row = (place_row >= 0) & (place_row < z.rows)
+        near_target = jnp.where(near_row[4:5, :] > 0, near_row[2:3, :], -1.0)
+        near_target = jnp.where(diag_row, place_row, near_target)
+        row_meta_ref[...] = jnp.full(row_meta_ref.shape, -1.0, F32)
+        row_meta_ref[0:1, 0 : z.near_rows] = near_target
+        row_meta_ref[1:2, 0 : z.far_rows] = far_target
+
+        place_col = (iota((z.near_rows, 1), 0) >> 1).astype(F32) - z.half
+        diag_col = (place_col >= 0) & (place_col < z.rows)
+        real = near_col[:, 4:5] > 0
+        first_source = near_col[:, 0:1] * z.first_rows + near_col[:, 1:2]
+        first_source = jnp.where(real, first_source, -1.0)
+        first_source = jnp.where(diag_col, mine * z.first_rows + place_col, first_source)
+        later_source = near_col[:, 0:1] * z.send_rows + near_col[:, 3:4]
+        later_source = jnp.where(real, later_source, -1.0)
+        later_source = jnp.where(
+            diag_col, z.devices * z.send_rows + place_col, later_source
         )
-    send_ref[pl.ds(z.info_row, z.devices, stride=z.first_rows), :] = info
-
+        lane = iota((z.near_rows, 128), 1)
+        near_meta_ref[...] = jnp.where(lane == 0, first_source, later_source)
+
+        def told(row_facts, col_facts, offset):
+            shape = (col_facts.shape[0], 128)
+            once = (iota(shape, 0) & 1) == 0
+            match = (fiota(shape, 1) == col_facts[:, 3:4] + offset) & once
+            told_value = jnp.where(match & (col_facts[:, 4:5] > 0), col_facts[:, 1:2] + 1.0, 0.0)
+            owner = fiota((z.devices, row_facts.shape[1]), 0)
+            return dot((owner == row_facts[0:1, :]).astype(BF16), told_value.astype(BF16))
+
+        info = told(near_row, near_col, 0) + told(far_row, far_col, z.slots)
+        for r in range(z.rows):
+            send_ref[pl.ds(r, z.devices, stride=z.first_rows), :] = jnp.broadcast_to(
+                defect[r : r + 1, :], (z.devices, width)
+            )
+        send_ref[pl.ds(z.info_row, z.devices, stride=z.first_rows), :] = info
+
+
+    describe()
     inputs = tile_inputs(far_source, defect)
     arrived = 0
     parts = []
@@ -316,7 +315,8 @@
             chunks[arrived].wait()
             arrived += 1
         for k in group:
-            store_tile(far_ref, k, tiles_ref[ids_ref[z.half + 1 + k]])
+            store_tile(far_ref, k, tiles_ref[ids_ref[z.half + k]])
+            near_list_ref[k] = tiles_ref[ids_ref[k]]
         parts.append(octet_products(far_ref, inputs, octet, z.half))
     while arrived < len(chunks):
         chunks[arrived].wait()
@@ -326,7 +326,6 @@
         send_ref[pl.ds(z.rows + s, z.devices, stride=z.first_rows), :] = pushes[
             s * z.devices : (s + 1) * z.devices
         ]
-    ids_copy.wait()
     mass_copy.wait()
     own_ref[1, 0 : z.rows, :] = mass_ref[...]
     diag_copy.wait()
@@ -358,26 +357,20 @@
 def first_kernel(
     z,
     received_ref,
-    tiles_ref,
-    diag_ref,
+    near_list_ref,
     far_ref,
     own_ref,
     row_meta_ref,
     near_meta_ref,
     far_meta_ref,
-    ids_in,
     send_ref,
     near_ref,
     state_ref,
     ask_ref,
     land_ref,
     scalar_ref,
-    ids_ref,
-    ids_sem,
 ):
     width = z.width
-    ids_copy = pltpu.make_async_copy(ids_in, ids_ref, ids_sem)
-    ids_copy.start()
     defect = own_ref[0]
     mass = own_ref[1]
     squares = jnp.zeros((z.devices, width), F32)
@@ -401,17 +394,11 @@
     land_ref[...] = land_mark
 
     inputs = tile_inputs(near_meta_ref[:, 0:1], received_ref[...])
-    octets = z.near_rows // (2 * OCTET)
-    parts = [None] * octets
-    waited = False
-    for octet in sorted(range(octets), key=lambda o: o < z.half // OCTET):
+    parts = []
+    for octet in range(z.near_rows // (2 * OCTET)):
         for k in range(OCTET * octet, min(OCTET * (octet + 1), z.near)):
-            if k < z.half and not waited:
-                ids_copy.wait()
-                waited = True
-            tile = tiles_ref[ids_ref[k]] if k < z.half else diag_ref[k - z.half]
-            store_tile(near_ref, k, tile)
-        parts[octet] = octet_products(near_ref, inputs, octet, z.near)
+            store_tile(near_ref, k, near_list_ref[k])
+        parts.append(octet_products(near_ref, inputs, octet, z.near))
     products = jnp.concatenate(parts, axis=0)
     image = mass * defect
     image = image + landed(z, received_ref, land_mark, z.rows, z.first_rows)
@@ -581,7 +568,7 @@
 
     rows_2d = tile_rows.reshape(1, z.tiles)
     cols_2d = tile_cols.reshape(1, z.tiles)
-    send, far, row_meta, near_meta, far_meta, own, ids, tiles, diag = call(
+    send, far, row_meta, near_meta, far_meta, own, near_list = call(
         prepare_kernel,
         "prepare",
         [hbm] * 7,
@@ -592,28 +579,28 @@
             shape(z.near_rows, 128),
             shape(z.far_rows, 128),
             shape(2, z.padded, width),
-            shape(2 * z.half + 2, dtype=jnp.int32),
-            shape(z.tiles, width, width),
-            shape(z.rows, width, width),
+            shape(z.near, width, width),
         ],
         [
-            pltpu.SMEM((2 * z.half + 2,), jnp.int32),
+            pltpu.VMEM((z.tiles, width, width), F32),
+            pltpu.SMEM((z.tiles,), jnp.int32),
             pltpu.SMEM((z.tiles,), jnp.int32),
             pltpu.VMEM((1, z.tiles), jnp.int32),
             pltpu.VMEM((1, z.tiles), jnp.int32),
             pltpu.VMEM((z.rows, width), F32),
             pltpu.VMEM((z.rows, width), F32),
             pltpu.VMEM((8, round_up(z.tiles, 128)), jnp.int32),
-            pltpu.SemaphoreType.DMA((6,)),
+            pltpu.SemaphoreType.DMA((5,)),
             pltpu.SemaphoreType.DMA((-(-z.tiles // CHUNK) + 1,)),
         ],
         map(in_hbm, (tile_rows, rows_2d, cols_2d, defect, mass, coupling, block_diag)),
+        z.tiles * width * width * 4 // MIB + 4,
     )
     received = exchange(z, send)
     send, near, state, ask, land, scalars = call(
         first_kernel,
         "first",
-        [vmem] * 9,
+        [vmem] * 7,
         [
             shape(z.devices * z.send_rows, width),
             pieces(z.near),
@@ -622,8 +609,8 @@
             shape(z.padded, z.cells, dtype=BF16),
             shape(8, 128),
         ],
-        [pltpu.SMEM((2 * z.half + 2,), jnp.int32), pltpu.SemaphoreType.DMA],
-        (received, tiles, diag, far, own, row_meta, near_meta, far_meta, ids),
+        [],
+        (received, near_list, far, own, row_meta, near_meta, far_meta),
     )
     received = exchange(z, send)
     send, state, scalars = call(

time: 55.8 us -> 55.6 us (level)
  no operation moved by 1% of the time
where the time goes in v4:
time: 55.6 us; the launch traced here: 55.4 us
  blocking collectives  45.3 us (81%)
  Pallas kernels  10.1 us (18%)
    all_to_all x4, blocking collectives, exchange(): lax.all_to_all(value, 'blk', split_axis=0, concat_axis=0, tiled=True)  45.3 us
    pallas_call x5, Pallas kernels, call(): pl.pallas_call(functools.partial(kernel, z), out_shape=outs, in_specs=ins...  10.1 us

profile of v4, /device:TPU:0, one launch (start us, length us, event | category | flops | bytes accessed | tf_op | source)
XLA Modules:
  0.0 55.4 jit_solution(6733792487645200617)
XLA Ops:
  0.0 4.2 %prepare.1 = (f32[480,128]{1,0:T(8,128)S(1)}, bf16[12288,128]{1,0:T(8,128)(2,1)S(1)}, f32[8,128]{1,0:T(8,128)S(1)}, f32[128,128]{1,0:T(8,128)S(1)}, f32[96,128]{...) custom-call(s32[96]{0:T(128)} %rows_hbm.1, s32[1,96]{1,0:T(1,128)} %bitcast.20, ...), custom_call_target="tpu_custom_call" | custom-call | tf_op jit(solution)/shard_map/prepare/pallas_call | solution.py:556
  4.3 17.4 %all_to_all.20 = f32[32,1,1920]{2,1,0:T(1,128)S(1)} all-to-all(f32[32,1,1920]{2,1,0:T(1,128)S(1)} %bitcast.15), channel_id=1, replica_groups=mesh['blk'=32] {'blk'}, dimensions={0} | all-to-all | bytes 491520 | tf_op jit(solution)/shard_map/all_to_all | solution.py:539
  21.6 2.5 %first.1 = (f32[160,128]{1,0:T(8,128)S(1)}, bf16[15360,128]{1,0:T(8,128)(2,1)S(1)}, f32[2,16,128]{2,1,0:T(8,128)S(1)}, bf16[64,16]{1,0:T(8,128)(2,1)S(1)}, bf16[...) custom-call(f32[480,128]{1,0:T(8,128)S(1)} %bitcast.12, f32[60,128,128]{2,1,0:T(8,128)S(1)} %get-tuple-element.25.near_list_ref, ...), custom_call_target="tpu_custom_call" | custom-call | tf_op jit(solution)/shard_map/first/pallas_call | solution.py:556
  24.2 9.7 %all_to_all.21 = f32[32,1,640]{2,1,0:T(1,128)S(1)} all-to-all(f32[32,1,640]{2,1,0:T(1,128)S(1)} %bitcast.17), channel_id=1, replica_groups=mesh['blk'=32] {'blk'}, dimensions={0} | all-to-all | bytes 163840 | tf_op jit(solution)/shard_map/all_to_all | solution.py:539
  33.9 1.7 %second.1 = (f32[160,128]{1,0:T(8,128)S(1)}, f32[4,16,128]{2,1,0:T(8,128)S(1)}, f32[8,128]{1,0:T(8,128)S(1)}) custom-call(f32[160,128]{1,0:T(8,128)S(1)} %bitcast.13, bf16[15360,128]{1,0:T(8,128)(2,1)S(1)} %get-tuple-element.32.near_ref, bf16[12288,128]{1,0:T(8,128)(2,1)S(1)} %get-tuple-element.26.far_ref, f32[2,16,128]{2,1,0:T(8,128)S(1)} %get-tuple-element.27.own_ref, ...), custom_call_target="tpu_custom_call" | custom-call | tf_op jit(solution)/shard_map/second/pallas_call | solution.py:556
  35.6 9.3 %all_to_all.22 = f32[32,1,640]{2,1,0:T(1,128)S(1)} all-to-all(f32[32,1,640]{2,1,0:T(1,128)S(1)} %bitcast.16), channel_id=1, replica_groups=mesh['blk'=32] {'blk'}, dimensions={0} | all-to-all | bytes 163840 | tf_op jit(solution)/shard_map/all_to_all | solution.py:539
  44.9 1.0 %third.1 = (f32[32,128]{1,0:T(8,128)S(1)}, f32[3,16,128]{2,1,0:T(8,128)S(1)}, f32[8,128]{1,0:T(8,128)S(1)}) custom-call(f32[160,128]{1,0:T(8,128)S(1)} %bitcast.14, bf16[15360,128]{1,0:T(8,128)(2,1)S(1)} %get-tuple-element.32.near_ref, f32[2,16,128]{2,1,0:T(8,128)S(1)} %get-tuple-element.27.own_ref, f32[8,128]{1,0:T(8,128)S(1)} %get-tuple-element.28.row_meta_ref, ...), custom_call_target="tpu_custom_call" | custom-call | tf_op jit(solution)/shard_map/third/pallas_call | solution.py:556
  45.8 8.9 %all_to_all.23 = f32[32,1,128]{2,1,0:T(1,128)S(1)} all-to-all(f32[32,1,128]{2,1,0:T(1,128)S(1)} %bitcast.19), channel_id=1, replica_groups=mesh['blk'=32] {'blk'}, dimensions={0} | all-to-all | bytes 32768 | tf_op jit(solution)/shard_map/all_to_all | solution.py:539
  54.7 0.7 %last.1 = f32[12,128]{1,0:T(8,128)} custom-call(f32[32,128]{1,0:T(8,128)S(1)} %bitcast.18, f32[3,16,128]{2,1,0:T(8,128)S(1)} %get-tuple-element.41.state_in, f32[8,128]{1,0:T(8,128)S(1)} %get-tuple-element.42.scalar_in), custom_call_target="tpu_custom_call" | custom-call | tf_op jit(solution)/shard_map/last/pallas_call | solution.py:556
